TPU v7x, 768 devices: a whole 4x8x12 slice. The times are simulated.
768 devices in a mesh: section: 4 (over x_lo, core), shard: 8 (over y), replica: 24 (over z, x_hi).
Axes of the slice: x: 4 (x_hi: 2, x_lo: 2; x = x_hi * 2 + x_lo), y: 8, z: 12, core: 2. Of those that a mesh axis runs over, the one named last changes fastest.
Arguments:
- acts_fwd: bfloat16 [4, 24576, 4096], P('section', ('shard', 'replica')), may hold values from -30 to 30
- pos_fwd: int32 [4, 24576], P('section', ('shard', 'replica')), may hold values from 0 to 2047
- saved_acts: bfloat16 [4, 24576, 4096], P('section', ('shard', 'replica')), may hold values from -30 to 30
- pos_bwd: int32 [4, 24576], P('section', ('shard', 'replica')), may hold values from 0 to 2047
- grads_in: bfloat16 [4, 24576, 4096], P('section', ('shard', 'replica')), may hold values from -6 to 6
- key_cotan: bfloat16 [4, 24576, 512], P('section', ('shard', 'replica')), may hold values from -6 to 6
- weight: bfloat16 [4, 4096, 512], P('section', 'shard'), may hold values from -0.09375 to 0.09375
- gain: float32 [4, 4096], P('section'), may hold values from 0.1 to 1.9
Outputs:
- keys: bfloat16 [4, 24576, 512], P('section', ('shard', 'replica'))
- grad_out: bfloat16 [4, 24576, 4096], P('section', ('shard', 'replica'))
- weight_grad: float32 [4, 4096, 512], P('section', 'shard')
All inputs are finite; a program needn't handle non-finite values.
Results may differ from a plain program's by a relative error of at most 0.0058.
Values may be sent and summed in bfloat16 or wider, within the bound.
No kernel may reach another device: no remote copies, remote signals or barrier semaphores. Data moves between devices by JAX's collectives and lax.ppermute only.
A program may use at most 64 MiB of HBM per device.

v0:
```python
import jax
import jax.numpy as jnp
from jax import lax
from jax.sharding import PartitionSpec as P

HEAD = 128


def from_behind(x, axis, by):
    size = lax.axis_size(axis)
    pairs = [(i, i + by) for i in range(size) if 0 <= i + by < size]
    return lax.ppermute(x, axis, pairs)


def rope_tables(positions):
    index = jnp.arange(HEAD // 2, dtype=jnp.float32)
    rate = 500000.0 ** (-(2.0 * index) / HEAD)
    angle = positions.astype(jnp.float32)[:, None] * rate[None, :]
    return (jnp.cos(angle), jnp.sin(angle))


def rotate(values, cosine, sine_part, orient):
    count = values.shape[0]
    heads = values.shape[1] // HEAD
    shaped = values.reshape(count, heads, HEAD)
    first_half = shaped[..., : HEAD // 2]
    second_half = shaped[..., HEAD // 2 :]
    cos_b = cosine[:, None, :]
    sin_b = orient * sine_part[:, None, :]
    joined = jnp.concatenate(
        [first_half * cos_b - second_half * sin_b, second_half * cos_b + first_half * sin_b], -1
    )
    return joined.reshape(count, heads * HEAD)


def normalize(stream, gain_row):
    values = stream.astype(jnp.float32)
    inverse = lax.rsqrt(jnp.mean(values * values, -1, keepdims=True) + 1e-05)
    return (values * inverse * gain_row[None, :], inverse, values)


def per_device(acts_fwd, pos_fwd, saved_acts, pos_bwd, grads_in, key_cotan, weight, gain):
    section_pos = lax.axis_index("section")
    section_count = lax.axis_size("section")
    came_fwd = from_behind(acts_fwd, "section", 1)
    stream = jnp.where(section_pos == 0, acts_fwd, came_fwd)[0]
    came_bwd = from_behind(grads_in, "section", -1)
    arrived = jnp.where(section_pos == section_count - 1, grads_in, came_bwd)[0]
    gain_row = gain[0]
    local_rows = weight[0]
    normed = normalize(stream, gain_row)[0].astype(jnp.bfloat16)
    back_f, inverse, saved_f = normalize(saved_acts[0], gain_row)
    back_normed = back_f.astype(jnp.bfloat16)
    cos_b, sin_b = rope_tables(pos_bwd[0])
    key_grad = rotate(key_cotan[0].astype(jnp.float32), cos_b, sin_b, -1.0).astype(jnp.bfloat16)
    tok_rows = normed.shape[0]
    gathered = lax.all_gather(local_rows, "shard", axis=0, tiled=True)
    projected = jnp.dot(normed, gathered, preferred_element_type=jnp.float32)
    normed_grad = lax.dot_general(
        key_grad, gathered, (((1,), (1,)), ((), ())), preferred_element_type=jnp.float32
    )
    cosine, sine_part = rope_tables(pos_fwd[0])
    keys = rotate(projected, cosine, sine_part, 1.0).astype(jnp.bfloat16)
    scaled = normed_grad * gain_row[None, :]
    stream_grad = inverse * scaled - saved_f * inverse**3 * jnp.mean(
        saved_f * scaled, -1, keepdims=True
    )
    grad_out = (arrived.astype(jnp.float32) + stream_grad).astype(jnp.bfloat16)
    shard_count = lax.axis_size("shard")
    replica_count = lax.axis_size("replica")
    term = lax.dot_general(
        back_normed, key_grad, (((0,), (0,)), ((), ())), preferred_element_type=jnp.float32
    )
    rounded = lax.optimization_barrier(term.astype(jnp.bfloat16))
    shard_sum = lax.psum_scatter(
        rounded.astype(jnp.float32), "shard", scatter_dimension=0, tiled=True
    )
    summed = lax.psum(shard_sum, "replica")
    token_total = tok_rows * shard_count * replica_count
    weight_grad = summed * float(token_total) ** (-0.5)
    return (keys[None], grad_out[None], weight_grad[None])


def solution(mesh):
    placed = (
        P("section", ("shard", "replica"), None),
        P("section", ("shard", "replica")),
        P("section", ("shard", "replica"), None),
        P("section", ("shard", "replica")),
        P("section", ("shard", "replica"), None),
        P("section", ("shard", "replica"), None),
        P("section", "shard", None),
        P("section", None),
    )
    return jax.shard_map(
        per_device,
        mesh=mesh,
        in_specs=placed,
        out_specs=(
            P("section", ("shard", "replica"), None),
            P("section", ("shard", "replica"), None),
            P("section", "shard", None),
        ),
        check_vma=False,
    )
```

profile of v0, /device:TPU:24, one launch (start us, length us, event | category | flops | bytes accessed | tf_op | source)
XLA Modules:
  0.0 439.9 jit_solution(793523997704315053)
XLA Ops:
  7.2 0.0 copy-start.1
  7.2 0.0 copy-start
  7.2 0.0 all-gather.3.cloned.1.call-start
  7.2 0.7 all-gather.3.cloned.1.call-update
  7.9 0.0 reduce-scatter.2.cloned.1.call-start
  8.0 1.0 reshape.210
  9.0 0.7 convert_bitcast_fusion.1
  9.7 0.3 multiply_cosine_fusion
  10.0 0.1 copy.13
  10.1 0.1 copy.12
  10.2 0.3 multiply_subtract_fusion
  10.5 0.2 maximum_convert_fusion
  10.6 65.8 %all-gather.3.cloned.1.call-done = bf16[1,4096,512]{2,1,0:T(8,128)(2,1)} async-done(((bf16[1,512,512]{2,1,0:T(8,128)(2,1)}), bf16[1,4096,512]{2,1,0:T(8,128)(2,1)}) %all-gather.3.cloned.1.call-update) | async-done | bytes 4194320 | tf_op jit(solution)/shard_map/all_gather | solution.py:57
  76.5 0.0 copy-done.1
  76.5 3.8 fusion.7
  80.3 1.4 convolution_convert_fusion
  81.7 4.4 %convert_element_type.113 = f32[4096,512]{1,0:T(8,128)} convert(bf16[4096,512]{1,0:T(8,128)(2,1)S(1)} %convolution_convert_fusion) | non-fusion elementwise | flops 2097152 | bytes 12582912 | tf_op jit(solution)/shard_map/convert_element_type | solution.py:76
  86.1 0.0 reduce-scatter.2.cloned.1.call-update
  86.1 0.0 all-reduce.2.cloned.1.call-start
  86.2 2.6 collective-permute-start
  88.7 1.3 collective-permute-start.1
  90.0 0.3 collective-permute-done
  90.4 1.6 fusion.4
  92.0 6.4 %copy.11 = bf16[512,4096]{1,0:T(8,128)(2,1)} copy(bf16[512,4096]{0,1:T(8,128)(2,1)} %bitcast.59) | data formatting | bytes 8388608 | tf_op jit(solution)/shard_map/dot_general | solution.py:58
  98.4 3.8 fusion.19
  102.3 0.8 copy.14
  103.1 82.2 %reduce-scatter.2.cloned.1.call-done = f32[512,512]{1,0:T(8,128)} async-done(((f32[4096,512]{1,0:T(8,128)}), f32[512,512]{1,0:T(8,128)}) %reduce-scatter.2.cloned.1.call-update) | async-done | bytes 1048592 | tf_op jit(solution)/shard_map/reduce_scatter | solution.py:75
  185.3 0.0 all-reduce.2.cloned.1.call-update
  185.4 0.0 collective-permute-done.1
  185.4 3.0 fusion.17
  188.4 242.6 %all-reduce.2.cloned.1.call-done = f32[512,512]{1,0:T(8,128)} async-done(((f32[512,512]{1,0:T(8,128)}), f32[512,512]{1,0:T(8,128)}) %all-reduce.2.cloned.1.call-update) | async-done | bytes 1048592 | tf_op jit(solution)/shard_map/psum | solution.py:78
  431.0 2.3 multiply_bitcast_fusion
  (7 shorter events, 0.1 us)
Async XLA Ops:
  7.2 69.3 %copy-start.1 = (f32[1,4096]{1,0:T(1,128)S(1)}, f32[1,4096]{1,0:T(1,128)}, u32[]{:S(2)}) copy-start(f32[1,4096]{1,0:T(1,128)} %param.15) | copy-start | bytes 49156
  7.2 69.3 %copy-start = (bf16[1,128,4096]{2,1,0:T(8,128)(2,1)S(1)}, bf16[1,128,4096]{2,1,0:T(8,128)(2,1)}, u32[]{:S(2)}) copy-start(bf16[1,128,4096]{2,1,0:T(8,128)(2,1)} %param.10) | copy-start | bytes 3145732
  7.2 69.3 %all-gather.3.cloned.1.call-start = ((), (), s32[]{:S(2)}) async-start(), calls=%async_computation.3 | async-start | bytes 4718592 | tf_op jit(solution)/shard_map/all_gather | solution.py:57
  7.9 177.4 %reduce-scatter.2.cloned.1.call-start = ((), (), s32[]{:S(2)}) async-start(), calls=%async_computation.1 | async-start | bytes 9437184 | tf_op jit(solution)/shard_map/reduce_scatter | solution.py:75
  86.1 344.9 %all-reduce.2.cloned.1.call-start = ((), (), s32[]{:S(2)}) async-start(), calls=%async_computation.2 | async-start | bytes 2097152 | tf_op jit(solution)/shard_map/psum | solution.py:78
  86.2 4.2 collective-permute-start
  88.7 96.6 %collective-permute-start.1 = (bf16[1,128,4096]{2,1,0:T(8,128)(2,1)}, bf16[1,128,4096]{2,1,0:T(8,128)(2,1)}, u32[]{:S(2)}, u32[]{:S(2)}) collective-permute-start(bf16[1,128,4096]{2,1,0:T(8,128)(2,1)} %param.12), channel_id=1, source_target_pairs={{192,0},{384,192},{576,384},{193,1},{385,193},{577,385},{194,2},{3... | collective-permute-start | bytes 3145736 | tf_op jit(solution)/shard_map/ppermute | solution.py:12
Sparse Core Ops, SparseCore 0:
  10.4 66.0 all-gather.2
  86.2 99.0 reduce-scatter.1
  188.6 242.4 all-reduce.1
where the time goes:
time: 441 us; the launch traced here: 440 us
  waiting for transfers between devices  392 us (89%)
  between operations  13.9 us (3%)
  other arithmetic  12.9 us (3%)
  matrix products  9 us (2%)
  local copies, waits for them, and re-layouts  8.37 us (2%)
    psum x1, waiting for transfers between devices, per_device(): summed = lax.psum(shard_sum, 'replica')  243 us
    reduce_scatter x1, waiting for transfers between devices, per_device(): lax.psum_scatter(rounded.astype(jnp.float32), 'shard', scatter_dimension=...  82.2 us
    all_gather x1, waiting for transfers between devices, per_device(): gathered = lax.all_gather(local_rows, 'shard', axis=0, tiled=True)  65.8 us
  transfers between devices with their start and end apart: 5, of which 4 were waited for; matrix products, arithmetic and copies ran while one was open for 4% of the time, Pallas kernels for 0%

commit v1 on v0

v1 whole, which is shorter than its diff:
```python
import jax
import jax.numpy as jnp
from jax import lax
from jax.sharding import PartitionSpec as P


HEAD = 128
LANES = 128


def from_behind(x, axis, by):
    size = lax.axis_size(axis)
    pairs = [(i, i + by) for i in range(size) if 0 <= i + by < size]
    return lax.ppermute(x, axis, pairs)


def rope_tables(positions):
    index = jnp.arange(HEAD // 2, dtype=jnp.float32)
    rate = 500000.0 ** (-(2.0 * index) / HEAD)
    angle = positions.astype(jnp.float32)[:, None] * rate[None, :]
    return (jnp.cos(angle), jnp.sin(angle))


def rotate(values, cosine, sine_part, orient):
    cos_full = jnp.concatenate([cosine, cosine], -1)
    sin_full = jnp.concatenate([-orient * sine_part, orient * sine_part], -1)
    heads = []
    for start in range(0, values.shape[1], HEAD):
        head = values[:, start : start + HEAD]
        swapped = jnp.concatenate([head[:, HEAD // 2 :], head[:, : HEAD // 2]], -1)
        heads.append(head * cos_full + swapped * sin_full)
    return jnp.concatenate(heads, -1)


def normalize(stream, gain_row):
    values = stream.astype(jnp.float32)
    inverse = lax.rsqrt(jnp.mean(values * values, -1, keepdims=True) + 1e-05)
    return (values * inverse * gain_row[None, :], inverse, values)


def swap_shards(rows):
    count = lax.axis_size("shard")
    tokens, width = rows.shape
    pieces = rows.reshape(tokens, count, width // count).transpose(1, 0, 2)
    return lax.all_to_all(pieces, "shard", split_axis=0, concat_axis=0).reshape(count * tokens, width // count)


def sum_over_replicas(term):
    rows, cols = term.shape
    count = lax.axis_size("replica")
    tall = term.astype(jnp.bfloat16).reshape(rows, cols // LANES, LANES).transpose(1, 0, 2).reshape(-1, LANES)
    total = tall.shape[0]
    piece = -(-total // (count * 8)) * 8
    tall = jnp.pad(tall, ((0, piece * count - total), (0, 0))).reshape(count, piece, LANES)
    got = lax.all_to_all(tall, "replica", split_axis=0, concat_axis=0)
    own = jnp.sum(got.astype(jnp.float32), 0).astype(jnp.bfloat16)
    full = lax.all_to_all(jnp.broadcast_to(own[None], (count, piece, LANES)), "replica", split_axis=0, concat_axis=0)
    full = full.reshape(count * piece, LANES)[:total].astype(jnp.float32)
    return full.reshape(cols // LANES, rows, LANES).transpose(1, 0, 2).reshape(rows, cols)


def per_device(acts_fwd, pos_fwd, saved_acts, pos_bwd, grads_in, key_cotan, weight, gain):
    section_pos = lax.axis_index("section")
    section_count = lax.axis_size("section")
    shard_count = lax.axis_size("shard")
    replica_count = lax.axis_size("replica")
    tok_rows = saved_acts.shape[1]
    gain_row = gain[0]
    local_rows = weight[0]
    saved_cols = swap_shards(saved_acts[0])
    saved_f = saved_acts[0].astype(jnp.float32)
    inverse = lax.rsqrt(jnp.mean(saved_f * saved_f, -1, keepdims=True) + 1e-05)
    cos_b, sin_b = rope_tables(pos_bwd[0])
    key_grad_f = rotate(key_cotan[0].astype(jnp.float32), cos_b, sin_b, -1.0)
    key_grad = key_grad_f.astype(jnp.bfloat16)
    own_keys, local_rows = lax.optimization_barrier(
        ((key_grad_f * inverse).astype(jnp.bfloat16), local_rows)
    )
    scaled_keys = lax.all_gather(own_keys, "shard", axis=0, tiled=True)
    gathered = lax.all_gather(local_rows, "shard", axis=0, tiled=True)
    term = lax.dot_general(
        saved_cols, scaled_keys, (((0,), (0,)), ((), ())), preferred_element_type=jnp.float32
    )
    summed = sum_over_replicas(term)
    own_rows = local_rows.shape[0]
    own_gain = lax.dynamic_slice(gain_row, (lax.axis_index("shard") * own_rows,), (own_rows,))
    token_total = tok_rows * shard_count * replica_count
    weight_grad = summed * (own_gain * float(token_total) ** (-0.5))[:, None]
    came_fwd = from_behind(acts_fwd, "section", 1)
    stream = jnp.where(section_pos == 0, acts_fwd, came_fwd)[0]
    came_bwd = from_behind(grads_in, "section", -1)
    arrived = jnp.where(section_pos == section_count - 1, grads_in, came_bwd)[0]
    normed = normalize(stream, gain_row)[0].astype(jnp.bfloat16)
    projected = jnp.dot(normed, gathered, preferred_element_type=jnp.float32)
    normed_grad = lax.dot_general(
        key_grad, gathered, (((1,), (1,)), ((), ())), preferred_element_type=jnp.float32
    )
    cosine, sine_part = rope_tables(pos_fwd[0])
    keys = rotate(projected, cosine, sine_part, 1.0).astype(jnp.bfloat16)
    scaled = normed_grad * gain_row[None, :]
    stream_grad = inverse * scaled - saved_f * inverse**3 * jnp.mean(
        saved_f * scaled, -1, keepdims=True
    )
    grad_out = (arrived.astype(jnp.float32) + stream_grad).astype(jnp.bfloat16)
    return (keys[None], grad_out[None], weight_grad[None])


def solution(mesh):
    placed = (
        P("section", ("shard", "replica"), None),
        P("section", ("shard", "replica")),
        P("section", ("shard", "replica"), None),
        P("section", ("shard", "replica")),
        P("section", ("shard", "replica"), None),
        P("section", ("shard", "replica"), None),
        P("section", "shard", None),
        P("section", None),
    )

    return jax.shard_map(
        per_device,
        mesh=mesh,
        in_specs=placed,
        out_specs=(
            P("section", ("shard", "replica"), None),
            P("section", ("shard", "replica"), None),
            P("section", "shard", None),
        ),
        check_vma=False,
    )
```

time: 441 us -> 155 us (0.35)
  the two profiles are of different devices: /device:TPU:24 before, /device:TPU:6 now
where the time goes in v1:
time: 155 us; the launch traced here: 154 us
  blocking collectives  77 us (50%)
  waiting for transfers between devices  27.3 us (18%)
  between operations  14.3 us (9%)
  starting transfers between devices  12.3 us (8%)
  other arithmetic  11.8 us (8%)
  matrix products  6.94 us (4%)
  local copies, waits for them, and re-layouts  4.4 us (3%)
    all_to_all x1, blocking collectives, swap_shards(): lax.all_to_all(pieces, 'shard', split_axis=0, concat_axis=0)  39.5 us
    all_to_all x1, blocking collectives, sum_over_replicas(): got = lax.all_to_all(tall, 'replica', split_axis=0, concat_axis=0)  37.5 us
    ppermute x2, waiting for transfers between devices, from_behind(): return lax.ppermute(x, axis, pairs)  14.4 us
    all_gather x1, waiting for transfers between devices, per_device(): scaled_keys = lax.all_gather(own_keys, 'shard', axis=0, tiled=True)  12.2 us
    all_to_all x1, starting transfers between devices, sum_over_replicas(): lax.all_to_all(jnp.broadcast_to(own[None], (count, piece, LANES)), 'repli...  6.69 us
    ppermute x2, starting transfers between devices, from_behind(): return lax.ppermute(x, axis, pairs)  5.57 us
    dot_general x1, matrix products, per_device(): projected = jnp.dot(normed, gathered, preferred_element_type=jnp.float32)  3.42 us
  transfers between devices with their start and end apart: 5, of which 2 were waited for; matrix products, arithmetic and copies ran while one was open for 10% of the time, Pallas kernels for 0%

profile of v1, /device:TPU:6, one launch (start us, length us, event | category | flops | bytes accessed | tf_op | source)
XLA Modules:
  0.0 154.1 jit_solution(12488695646564862432)
XLA Ops:
  7.3 1.0 bitcast_convert_fusion
  8.3 0.1 fusion.35
  8.5 0.3 fusion.3
  8.7 0.6 multiply_multiply_fusion
  9.3 1.2 broadcast_multiply_fusion
  10.6 0.1 fusion.27
  10.8 0.7 multiply_convert_fusion
  11.6 0.7 all-gather.3.cloned.1.call-update
  12.3 0.7 copy.12
  13.0 39.5 %all_to_all.15 = bf16[8,128,512]{1,2,0:T(8,128)(2,1)S(1)} all-to-all(bf16[8,128,512]{1,2,0:T(8,128)(2,1)S(1)} %bitcast.57), channel_id=1, replica_groups=mesh['section'=4,'shard'=8,'replica'=24] {'shard'}, dimensions={0} | all-to-all | bytes 2097152 | tf_op jit(solution)/shard_map/all_to_all | solution.py:45
  52.5 0.5 copy.13
  53.0 12.2 %all-gather.5.cloned.1.call-done = bf16[1024,512]{1,0:T(8,128)(2,1)} async-done(((bf16[128,512]{1,0:T(8,128)(2,1)}), bf16[1024,512]{1,0:T(8,128)(2,1)}) %all-gather.5.cloned.1.call-update) | async-done | bytes 1048592 | tf_op jit(solution)/shard_map/all_gather | solution.py:79
  65.2 1.9 %convolution_convert_fusion = bf16[512,512]{1,0:T(8,128)(2,1)S(1)} fusion(bf16[1024,512]{1,0:T(8,128)(2,1)} %all-gather.5.cloned.1.call-done, bf16[1024,512]{1,0:T(8,128)(2,1)S(1)} %bitcast.62), kind=kOutput, calls=%fused_computation.15 | convolution fusion | flops 537133056 | bytes 2621440 | tf_op jit(solution)/shard_map/dot_general | solution.py:81
  67.1 0.3 copy.14
  67.5 37.5 %all_to_all.16 = bf16[24,88,128]{2,1,0:T(8,128)(2,1)S(1)} all-to-all(bf16[24,88,128]{2,1,0:T(8,128)(2,1)S(1)} %bitcast.58), channel_id=1, replica_groups=mesh['section'=4,'shard'=8,'replica'=24] {'replica'}, dimensions={0} | all-to-all | bytes 1081344 | tf_op jit(solution)/shard_map/all_to_all | solution.py:55
  105.0 0.9 broadcast_in_dim.5
  105.9 6.7 %all-to-all-start.2 = ((bf16[24,88,128]{2,1,0:T(8,128)(2,1)}), bf16[24,88,128]{2,1,0:T(8,128)(2,1)S(1)}, u32[]{:S(2)}, u32[]{:S(2)}) async-start(bf16[24,88,128]{2,1,0:T(8,128)(2,1)} %broadcast_in_dim.5), calls=%async_computation.2 | async-start | bytes 1081344 | tf_op jit(solution)/shard_map/all_to_all | solution.py:57
  112.6 1.9 %collective-permute-start = (bf16[1,128,4096]{2,1,0:T(8,128)(2,1)S(1)}, bf16[1,128,4096]{2,1,0:T(8,128)(2,1)}, u32[]{:S(2)}, u32[]{:S(2)}) collective-permute-start(bf16[1,128,4096]{2,1,0:T(8,128)(2,1)S(1)} %copy-done.2), channel_id=1, source_target_pairs={{0,192},{192,384},{384,576},{1,193},{193,385},{385,577},{2,194},{1... | collective-permute-start | bytes 3145736 | tf_op jit(solution)/shard_map/ppermute | solution.py:14
  114.6 3.6 %collective-permute-start.1 = (bf16[1,128,4096]{2,1,0:T(8,128)(2,1)}, bf16[1,128,4096]{2,1,0:T(8,128)(2,1)}, u32[]{:S(2)}, u32[]{:S(2)}) collective-permute-start(bf16[1,128,4096]{2,1,0:T(8,128)(2,1)} %param.12), channel_id=1, source_target_pairs={{192,0},{384,192},{576,384},{193,1},{385,193},{577,385},{194,2},{3... | collective-permute-start | bytes 3145736 | tf_op jit(solution)/shard_map/ppermute | solution.py:14
  118.2 0.6 dynamic-slice_multiply_fusion
  118.8 14.4 %collective-permute-done = bf16[1,128,4096]{2,1,0:T(8,128)(2,1)} collective-permute-done((bf16[1,128,4096]{2,1,0:T(8,128)(2,1)S(1)}, bf16[1,128,4096]{2,1,0:T(8,128)(2,1)}, u32[]{:S(2)}, u32[]{:S(2)}) %collective-permute-start) | collective-permute-done | bytes 1048608 | tf_op jit(solution)/shard_map/ppermute | solution.py:14
  133.2 1.6 %fusion = f32[128]{0:T(128)S(1)} fusion(bf16[1,128,4096]{2,1,0:T(8,128)(2,1)S(1)} %copy-done.2, bf16[1,128,4096]{2,1,0:T(8,128)(2,1)} %collective-permute-done, pred[]{:T(512)S(6)} %eq.6), kind=kLoop, calls=%fused_computation.6 | loop fusion | flops 2097024 | bytes 2097665 | tf_op jit(solution)/shard_map/reduce_sum | solution.py:37
  134.8 0.6 add_rsqrt_fusion.1
  135.6 0.3 copy.15
  135.9 0.8 bitcast_multiply_fusion
  136.7 1.3 copy.16
  138.0 3.4 %fusion.10 = f32[128,512]{1,0:T(8,128)S(1)} fusion(bf16[4096,512]{1,0:T(8,128)(2,1)} %all-gather.3.cloned.1.call-done, f32[4096]{0:T(1024)S(1)} %bitcast.65, f32[128]{0:T(128)} %add_rsqrt_fusion.1, bf16[1,128,4096]{2,1,0:T(8,128)(2,1)S(1)} %copy-done.3, bf16[1,128,4096]{2,1,0:T(8,128)(2,1)} %collective-permute-done, pred[]{:T(512)S(6)} %eq.6), kind=kOutput, calls=%fused_computation.17 | convolution fusion | flops 539492352 | bytes 6570497 | tf_op jit(solution)/shard_map/dot_general | solution.py:94
  141.5 0.1 fusion.34
  141.8 0.1 fusion.30
  141.9 0.7 pad_maximum_fusion.1
  142.6 1.6 %fusion.8 = (f32[128]{0:T(128)S(1)}, f32[128,4096]{1,0:T(8,128)S(1)}) fusion(bf16[1,128,4096]{2,1,0:T(8,128)(2,1)S(1)} %copy-done, f32[4096]{0:T(1024)S(1)} %bitcast.66, bf16[4096,512]{1,0:T(8,128)(2,1)S(1)} %copy-done.1, f32[128,128]{1,0:T(8,128)S(1)} %get-tuple-element.18, f32[128,128]{1,0:T(8,128)S(1)} %get-tuple-element.19, ...), kind=kOutput, calls=%fused_computation.14 | convolution fusion | flops 539492224 | bytes 7619072 | tf_op jit(solution)/shard_map/dot_general | solution.py:95
  144.2 3.0 %fusion.9 = bf16[1,128,4096]{2,1,0:T(8,128)(2,1)} fusion(f32[128,4096]{1,0:T(8,128)S(1)} %get-tuple-element.48, bf16[1,128,4096]{2,1,0:T(8,128)(2,1)S(1)} %copy-done, f32[128]{0:T(128)S(1)} %broadcast_multiply_fusion.2, f32[128]{0:T(128)S(1)} %copy-done.9, f32[128]{0:T(128)S(1)} %copy-done.8, bf16[1,128,4096]{2,1,0:T(8,128)(2,1)S(1)} %copy-done.4, ...), kind=kLoop, calls=%fused_computation.16 | loop fusion | flops 4718592 | bytes 6292993 | tf_op jit(solution)/shard_map/broadcast_in_dim | solution.py:105
  (39 shorter events, 0.7 us)
Async XLA Ops:
  7.2 1.3 copy-start
  7.2 2.1 %copy-start.10 = (s32[1,128]{1,0:T(1,128)S(1)}, s32[1,128]{1,0:T(1,128)}, u32[]{:S(2)}) copy-start(s32[1,128]{1,0:T(1,128)} %param.9) | copy-start | bytes 1540
  7.2 2.1 %copy-start.11 = (s32[1,128]{1,0:T(1,128)S(1)}, s32[1,128]{1,0:T(1,128)}, u32[]{:S(2)}) copy-start(s32[1,128]{1,0:T(1,128)} %param.11) | copy-start | bytes 1540
  7.2 58.0 %all-gather.5.cloned.1.call-start = ((), (), s32[]{:S(2)}) async-start(), calls=%async_computation.4 | async-start | bytes 1179648 | tf_op jit(solution)/shard_map/all_gather | solution.py:79
  9.3 3.6 %copy-start.7 = (f32[128]{0:T(128)}, f32[128]{0:T(128)S(1)}, u32[]{:S(2)}) copy-start(f32[128]{0:T(128)S(1)} %get-tuple-element.43) | copy-start | bytes 1540
  11.5 126.5 %all-gather.3.cloned.1.call-start = ((), (), s32[]{:S(2)}) async-start(), calls=%async_computation.3 | async-start | bytes 4718592 | tf_op jit(solution)/shard_map/all_gather | solution.py:80
  67.4 45.2 %copy-start.2 = (bf16[1,128,4096]{2,1,0:T(8,128)(2,1)S(1)}, bf16[1,128,4096]{2,1,0:T(8,128)(2,1)}, u32[]{:S(2)}) copy-start(bf16[1,128,4096]{2,1,0:T(8,128)(2,1)} %param.8) | copy-start | bytes 3145732
  67.4 50.8 %copy-start.6 = (f32[1,4096]{1,0:T(1,128)S(1)}, f32[1,4096]{1,0:T(1,128)}, u32[]{:S(2)}) copy-start(f32[1,4096]{1,0:T(1,128)} %param.15) | copy-start | bytes 49156
  105.9 29.5 %all-to-all-start.2 = ((bf16[24,88,128]{2,1,0:T(8,128)(2,1)}), bf16[24,88,128]{2,1,0:T(8,128)(2,1)S(1)}, u32[]{:S(2)}, u32[]{:S(2)}) async-start(bf16[24,88,128]{2,1,0:T(8,128)(2,1)} %broadcast_in_dim.5), calls=%async_computation.2 | async-start | bytes 1081344 | tf_op jit(solution)/shard_map/all_to_all | solution.py:57
  112.6 20.6 %collective-permute-start = (bf16[1,128,4096]{2,1,0:T(8,128)(2,1)S(1)}, bf16[1,128,4096]{2,1,0:T(8,128)(2,1)}, u32[]{:S(2)}, u32[]{:S(2)}) collective-permute-start(bf16[1,128,4096]{2,1,0:T(8,128)(2,1)S(1)} %copy-done.2), channel_id=1, source_target_pairs={{0,192},{192,384},{384,576},{1,193},{193,385},{385,577},{2,194},{1... | collective-permute-start | bytes 3145736 | tf_op jit(solution)/shard_map/ppermute | solution.py:14
  114.6 29.6 %collective-permute-start.1 = (bf16[1,128,4096]{2,1,0:T(8,128)(2,1)}, bf16[1,128,4096]{2,1,0:T(8,128)(2,1)}, u32[]{:S(2)}, u32[]{:S(2)}) collective-permute-start(bf16[1,128,4096]{2,1,0:T(8,128)(2,1)} %param.12), channel_id=1, source_target_pairs={{192,0},{384,192},{576,384},{193,1},{385,193},{577,385},{194,2},{3... | collective-permute-start | bytes 3145736 | tf_op jit(solution)/shard_map/ppermute | solution.py:14
  136.7 1.3 copy-start.3
  138.0 3.6 %copy-start.5 = (f32[128,64]{1,0:T(8,128)S(1)}, f32[128,64]{1,0:T(8,128)}, u32[]{:S(2)}) copy-start(f32[128,64]{1,0:T(8,128)} %get-tuple-element.38) | copy-start | bytes 98308
  138.0 4.5 %copy-start.1 = (bf16[4096,512]{1,0:T(8,128)(2,1)S(1)}, bf16[4096,512]{1,0:T(8,128)(2,1)}, u32[]{:S(2)}) copy-start(bf16[4096,512]{1,0:T(8,128)(2,1)} %all-gather.3.cloned.1.call-done) | copy-start | bytes 12582916
  142.6 1.6 %copy-start.4 = (bf16[1,128,4096]{2,1,0:T(8,128)(2,1)S(1)}, bf16[1,128,4096]{2,1,0:T(8,128)(2,1)}, u32[]{:S(2)}) copy-start(bf16[1,128,4096]{2,1,0:T(8,128)(2,1)} %param.12) | copy-start | bytes 3145732
  142.6 1.6 %copy-start.8 = (f32[128]{0:T(128)S(1)}, f32[128]{0:T(128)}, u32[]{:S(2)}) copy-start(f32[128]{0:T(128)} %copy-done.7) | copy-start | bytes 1540
  142.6 1.6 %copy-start.9 = (f32[128]{0:T(128)S(1)}, f32[128]{0:T(128)}, u32[]{:S(2)}) copy-start(f32[128]{0:T(128)} %get-tuple-element.42) | copy-start | bytes 1540
Sparse Core Ops, SparseCore 0:
  11.7 53.4 all-gather.4
  67.6 61.4 all-gather.2

commit v2 on v0

v2 whole, which is shorter than its diff:
```python
import jax
import jax.numpy as jnp
from jax import lax
from jax.experimental import pallas as pl
from jax.experimental.pallas import tpu as pltpu
from jax.sharding import PartitionSpec as P


HEAD = 128
LANES = 128
EPS = 1e-05
F32 = jnp.float32
BF16 = jnp.bfloat16


def from_behind(x, axis, by):
    size = lax.axis_size(axis)
    pairs = [(i, i + by) for i in range(size) if 0 <= i + by < size]
    return lax.ppermute(x, axis, pairs)


def rope_tables(positions):
    index = jnp.arange(HEAD // 2, dtype=F32)
    rate = 500000.0 ** (-(2.0 * index) / HEAD)
    rate = jnp.concatenate([rate, rate])
    sign = jnp.where(jnp.arange(HEAD) < HEAD // 2, -1.0, 1.0).astype(F32)
    angle = positions.astype(F32)[:, None] * rate[None, :]
    return jnp.cos(angle), jnp.sin(angle) * sign[None, :]


def turn(head, cosine, sine_part):
    return head * cosine + pltpu.roll(head, HEAD // 2, 1) * sine_part


def keys_kernel(saved_ref, cotan_ref, cos_ref, sin_ref, grad_ref, scaled_ref):
    saved = saved_ref[...].astype(F32)
    inverse = lax.rsqrt(jnp.mean(saved * saved, -1, keepdims=True) + EPS)
    cosine = cos_ref[...]
    sine_part = -sin_ref[...]
    for start in range(0, cotan_ref.shape[1], HEAD):
        span = pl.ds(start, HEAD)
        turned = turn(cotan_ref[:, span].astype(F32), cosine, sine_part)
        grad_ref[:, span] = turned.astype(BF16)
        scaled_ref[:, span] = (turned * inverse).astype(BF16)


def key_factors(saved, cotan, cosine, sine_part):
    shape = jax.ShapeDtypeStruct(cotan.shape, BF16)
    return pl.pallas_call(keys_kernel, out_shape=(shape, shape), name="key_factors")(saved, cotan, cosine, sine_part)


def term_kernel(shard_ref, saved_ref, *rest):
    *key_refs, out_ref, acc_ref = rest
    count = saved_ref.shape[0]
    for place, key_ref in enumerate(key_refs):
        distance, first = RING[place]
        block = lax.rem(shard_ref[0] + count - distance, count)
        part = saved_ref[block, pl.ds(first, key_ref.shape[0]), :]
        term = lax.dot_general(part, key_ref[...], (((0,), (0,)), ((), ())), preferred_element_type=F32)
        if place == 0:
            acc_ref[...] = term
        else:
            acc_ref[...] += term
    rows, cols = acc_ref.shape
    for block in range(cols // LANES):
        out_ref[pl.ds(block * rows, rows), :] = acc_ref[:, pl.ds(block * LANES, LANES)].astype(BF16)
    used = rows * cols // LANES
    if used < out_ref.shape[0]:
        out_ref[pl.ds(used, out_ref.shape[0] - used), :] = jnp.zeros((out_ref.shape[0] - used, LANES), BF16)


RING = ((0, 0), (1, 0), (7, 0), (2, 0), (6, 0), (3, 0), (5, 0), (4, 0), (4, 64))


def ring_blocks(rows):
    count = lax.axis_size("shard")
    right = [(i, (i + 1) % count) for i in range(count)]
    left = [(i, (i - 1) % count) for i in range(count)]
    blocks = [rows]
    came_right = came_left = rows
    for _ in range(count // 2 - 1):
        came_right = lax.ppermute(came_right, "shard", right)
        came_left = lax.ppermute(came_left, "shard", left)
        blocks += [came_right, came_left]
    half = rows.shape[0] // 2
    blocks.append(lax.ppermute(came_right[:half], "shard", right))
    blocks.append(lax.ppermute(came_left[half:], "shard", left))
    return blocks


def local_term(saved_cols, keys, shard, tall):
    rows = saved_cols.shape[2]
    cols = keys[0].shape[1]
    vmem = pl.BlockSpec(memory_space=pltpu.VMEM)
    return pl.pallas_call(
        term_kernel,
        in_specs=[pl.BlockSpec(memory_space=pltpu.SMEM)] + [vmem] * (1 + len(keys)),
        out_specs=vmem,
        out_shape=jax.ShapeDtypeStruct((tall, LANES), BF16),
        scratch_shapes=[pltpu.VMEM((rows, cols), F32)],
        name="local_term",
    )(shard, saved_cols, *keys)


def sum_kernel(got_ref, out_ref):
    total = jnp.sum(got_ref[...].astype(F32), 0).astype(BF16)
    out_ref[...] = jnp.broadcast_to(total[None], out_ref.shape)


def sum_pieces(got):
    return pl.pallas_call(sum_kernel, out_shape=jax.ShapeDtypeStruct(got.shape, BF16), name="sum_pieces")(got)


def spread_kernel(full_ref, scale_ref, out_ref):
    rows, cols = out_ref.shape
    scale = scale_ref[...]
    for block in range(cols // LANES):
        out_ref[:, pl.ds(block * LANES, LANES)] = full_ref[pl.ds(block * rows, rows), :].astype(F32) * scale


def spread(full, scale, rows, cols):
    return pl.pallas_call(spread_kernel, out_shape=jax.ShapeDtypeStruct((rows, cols), F32), name="spread")(full, scale)


def window_kernel(
    weight_ref, acts_ref, came_fwd_ref, saved_ref, grads_ref, came_bwd_ref, key_grad_ref, gain_ref, cos_ref, sin_ref,
    place_ref, keys_ref, grad_out_ref, normed_ref, proj_ref, ng_ref,
):
    step = pl.program_id(0)
    block = weight_ref.shape[0]
    span = pl.ds(pl.multiple_of(step * block, block), block)

    @pl.when(step == 0)
    def _():
        stream = jnp.where(place_ref[0] == 0, acts_ref[...], came_fwd_ref[...]).astype(F32)
        inverse = lax.rsqrt(jnp.mean(stream * stream, -1, keepdims=True) + EPS)
        normed_ref[...] = (stream * inverse * gain_ref[...]).astype(BF16)
        proj_ref[...] = jnp.zeros_like(proj_ref)

    rows = weight_ref[...]
    proj_ref[...] += jnp.dot(normed_ref[:, span], rows, preferred_element_type=F32)
    ng_ref[:, span] = (
        lax.dot_general(key_grad_ref[...], rows, (((1,), (1,)), ((), ())), preferred_element_type=F32)
        * gain_ref[:, span]
    )

    @pl.when(step == pl.num_programs(0) - 1)
    def _():
        cosine = cos_ref[...]
        sine_part = sin_ref[...]
        for start in range(0, keys_ref.shape[1], HEAD):
            head = pl.ds(start, HEAD)
            keys_ref[:, head] = turn(proj_ref[:, head], cosine, sine_part).astype(BF16)
        saved = saved_ref[...].astype(F32)
        inverse = lax.rsqrt(jnp.mean(saved * saved, -1, keepdims=True) + EPS)
        scaled = ng_ref[...]
        pull = inverse * inverse * inverse * jnp.mean(saved * scaled, -1, keepdims=True)
        arrived = jnp.where(place_ref[1] == 0, grads_ref[...], came_bwd_ref[...]).astype(F32)
        grad_out_ref[...] = (arrived + (inverse * scaled - saved * pull)).astype(BF16)


def window(weight, acts, came_fwd, saved, grads, came_bwd, key_grad, gain_row, cosine, sine_part, place):
    tokens, width = acts.shape
    cols = weight.shape[2]
    block = width // weight.shape[0]
    whole = lambda *shape: pl.BlockSpec(shape, lambda i: (0,) * len(shape))
    return pl.pallas_call(
        window_kernel,
        grid=(width // block,),
        in_specs=[
            pl.BlockSpec((None, block, cols), lambda i: (i, 0, 0)),
            whole(tokens, width), whole(tokens, width), whole(tokens, width), whole(tokens, width), whole(tokens, width),
            whole(tokens, cols), whole(1, width), whole(tokens, HEAD), whole(tokens, HEAD),
            pl.BlockSpec(memory_space=pltpu.SMEM),
        ],
        out_specs=(whole(tokens, cols), whole(tokens, width)),
        out_shape=(jax.ShapeDtypeStruct((tokens, cols), BF16), jax.ShapeDtypeStruct((tokens, width), BF16)),
        scratch_shapes=[pltpu.VMEM((tokens, width), BF16), pltpu.VMEM((tokens, cols), F32), pltpu.VMEM((tokens, width), F32)],
        name="window",
    )(weight, acts, came_fwd, saved, grads, came_bwd, key_grad, gain_row, cosine, sine_part, place)


def per_device(acts_fwd, pos_fwd, saved_acts, pos_bwd, grads_in, key_cotan, weight, gain):
    section_pos = lax.axis_index("section")
    section_count = lax.axis_size("section")
    shard_count = lax.axis_size("shard")
    replica_count = lax.axis_size("replica")
    _, tok_rows, _ = saved_acts.shape
    own_rows, cols = weight.shape[1:]
    gain_row = gain[0]
    pieces = saved_acts[0].reshape(tok_rows, shard_count, own_rows).transpose(1, 0, 2)
    saved_cols = lax.all_to_all(pieces, "shard", split_axis=0, concat_axis=0)
    cos_b, sin_b = rope_tables(pos_bwd[0])
    key_grad, own_keys = key_factors(saved_acts[0], key_cotan[0], cos_b, sin_b)
    ring_keys = ring_blocks(own_keys)
    share = -(-own_rows // (replica_count * 8)) * 8
    padded = jnp.pad(weight[0], ((0, share * replica_count - own_rows), (0, 0)))
    mine = lax.dynamic_slice(padded, (lax.axis_index("replica") * share, 0), (share, cols))
    gathered = lax.all_gather(mine, ("shard", "replica"), axis=0, tiled=True)
    gathered = gathered.reshape(shard_count, share * replica_count, cols)
    total = own_rows * cols // LANES
    piece = -(-total // (replica_count * 8)) * 8
    shard = lax.axis_index("shard").astype(jnp.int32)[None]
    tall = local_term(saved_cols, ring_keys, shard, piece * replica_count)
    got = lax.all_to_all(tall.reshape(replica_count, piece, LANES), "replica", split_axis=0, concat_axis=0)
    own = sum_pieces(got)
    full = lax.all_to_all(own, "replica", split_axis=0, concat_axis=0).reshape(-1, LANES)
    token_total = tok_rows * shard_count * replica_count
    own_gain = lax.dynamic_slice(gain_row, (lax.axis_index("shard") * own_rows,), (own_rows,))
    scale = jnp.broadcast_to((own_gain * float(token_total) ** (-0.5))[:, None], (own_rows, LANES))
    weight_grad = spread(full, scale, own_rows, cols)
    came_fwd = from_behind(acts_fwd[0], "section", 1)
    came_bwd = from_behind(grads_in[0], "section", -1)
    cos_f, sin_f = rope_tables(pos_fwd[0])
    place = jnp.stack([section_pos, section_count - 1 - section_pos]).astype(jnp.int32)
    keys, grad_out = window(
        gathered, acts_fwd[0], came_fwd, saved_acts[0], grads_in[0], came_bwd, key_grad, gain_row[None], cos_f, sin_f, place
    )
    return (keys[None], grad_out[None], weight_grad[None])


def solution(mesh):
    rows3 = P("section", ("shard", "replica"), None)
    rows2 = P("section", ("shard", "replica"))

    return jax.shard_map(
        per_device,
        mesh=mesh,
        in_specs=(rows3, rows2, rows3, rows2, rows3, rows3, P("section", "shard", None), P("section", None)),
        out_specs=(rows3, rows3, P("section", "shard", None)),
        check_vma=False,
    )
```

time: 441 us -> 244 us (0.55)
  the two profiles are of different devices: /device:TPU:24 before, /device:TPU:8 now
where the time goes in v2:
time: 244 us
  waiting for transfers between devices  108 us (44%)
  starting transfers between devices  49 us (20%)
  blocking collectives  40.9 us (17%)
  Pallas kernels  21 us (9%)
  between operations  14.2 us (6%)
  local copies, waits for them, and re-layouts  7.47 us (3%)
  other arithmetic  2.61 us (1%)
    all_gather x1, waiting for transfers between devices, per_device(): gathered = lax.all_gather(mine, ('shard', 'replica'), axis=0, tiled=True)  73.8 us
    all_to_all x1, blocking collectives, per_device(): lax.all_to_all(tall.reshape(replica_count, piece, LANES), 'replica', spli...  40.9 us
    all_to_all x1, waiting for transfers between devices, per_device(): lax.all_to_all(own, 'replica', split_axis=0, concat_axis=0)  18.8 us
    all_to_all x1, starting transfers between devices, per_device(): saved_cols = lax.all_to_all(pieces, 'shard', split_axis=0, concat_axis=0)  13 us
    ppermute x3, waiting for transfers between devices, ring_blocks(): came_right = lax.ppermute(came_right, 'shard', right)  11.8 us
    pallas_call x1, Pallas kernels, window(): pl.pallas_call(window_kernel, grid=(width // block,), in_specs=[pl.BlockS...  10.8 us
    ppermute x3, starting transfers between devices, ring_blocks(): came_right = lax.ppermute(came_right, 'shard', right)  9.83 us
    ppermute x3, starting transfers between devices, ring_blocks(): came_left = lax.ppermute(came_left, 'shard', left)  9.52 us
  transfers between devices with their start and end apart: 13, of which 8 were waited for; matrix products, arithmetic and copies ran while one was open for 3% of the time, Pallas kernels for 4%

profile of v2, /device:TPU:8, one launch (start us, length us, event | category | flops | bytes accessed | tf_op | source)
XLA Modules:
  0.0 243.5 jit_solution(1853370781592997906)
XLA Ops:
  7.2 1.3 pad_dynamic-slice_fusion
  8.6 1.6 copy.11
  10.2 1.3 copy.12
  11.6 13.0 %all-to-all-start = ((bf16[8,128,512]{2,1,0:T(8,128)(2,1)}), bf16[8,128,512]{2,1,0:T(8,128)(2,1)S(1)}, u32[]{:S(2)}, u32[]{:S(2)}) async-start(bf16[8,128,512]{2,1,0:T(8,128)(2,1)} %bitcast.14), calls=%async_computation | async-start | bytes 2097152 | tf_op jit(solution)/shard_map/all_to_all | solution.py:192
  24.7 1.2 fusion.1
  25.9 2.3 key_factors.1
  28.2 3.4 %collective-permute-start.2 = (bf16[128,512]{1,0:T(8,128)(2,1)}, bf16[128,512]{1,0:T(8,128)(2,1)S(1)}, u32[]{:S(2)}, u32[]{:S(2)}) collective-permute-start(bf16[128,512]{1,0:T(8,128)(2,1)} %get-tuple-element.10.rest_0_), channel_id=1, source_target_pairs={{0,24},{24,48},{48,72},{72,96},{96,120},{120,144},{144,168},{168,0... | collective-permute-start | bytes 393224 | tf_op jit(solution)/shard_map/ppermute | solution.py:82
  31.6 2.5 %collective-permute-start.3 = (bf16[128,512]{1,0:T(8,128)(2,1)}, bf16[128,512]{1,0:T(8,128)(2,1)S(1)}, u32[]{:S(2)}, u32[]{:S(2)}) collective-permute-start(bf16[128,512]{1,0:T(8,128)(2,1)} %get-tuple-element.10.rest_0_), channel_id=1, source_target_pairs={{0,168},{24,0},{48,24},{72,48},{96,72},{120,96},{144,120},{168,144... | collective-permute-start | bytes 393224 | tf_op jit(solution)/shard_map/ppermute | solution.py:83
  34.1 9.8 %collective-permute-done.2.rest_1_ = bf16[128,512]{1,0:T(8,128)(2,1)S(1)} collective-permute-done((bf16[128,512]{1,0:T(8,128)(2,1)}, bf16[128,512]{1,0:T(8,128)(2,1)S(1)}, u32[]{:S(2)}, u32[]{:S(2)}) %collective-permute-start.2) | collective-permute-done | bytes 131104 | tf_op jit(solution)/shard_map/ppermute | solution.py:82
  43.9 3.8 %collective-permute-start.4 = (bf16[128,512]{1,0:T(8,128)(2,1)S(1)}, bf16[128,512]{1,0:T(8,128)(2,1)S(1)}, u32[]{:S(2)}, u32[]{:S(2)}) collective-permute-start(bf16[128,512]{1,0:T(8,128)(2,1)S(1)} %collective-permute-done.2.rest_1_), channel_id=1, source_target_pairs={{0,24},{24,48},{48,72},{72,96},{96,120},{120,144},{144,168},{168,0... | collective-permute-start | bytes 393224 | tf_op jit(solution)/shard_map/ppermute | solution.py:82
  47.7 3.1 %collective-permute-start.5 = (bf16[128,512]{1,0:T(8,128)(2,1)S(1)}, bf16[128,512]{1,0:T(8,128)(2,1)S(1)}, u32[]{:S(2)}, u32[]{:S(2)}) collective-permute-start(bf16[128,512]{1,0:T(8,128)(2,1)S(1)} %collective-permute-done.3.rest_2_), channel_id=1, source_target_pairs={{0,168},{24,0},{48,24},{72,48},{96,72},{120,96},{144,120},{168,144... | collective-permute-start | bytes 393224 | tf_op jit(solution)/shard_map/ppermute | solution.py:83
  50.8 1.0 collective-permute-done.4.rest_3_
  51.8 2.7 %collective-permute-start.6 = (bf16[128,512]{1,0:T(8,128)(2,1)S(1)}, bf16[128,512]{1,0:T(8,128)(2,1)S(1)}, u32[]{:S(2)}, u32[]{:S(2)}) collective-permute-start(bf16[128,512]{1,0:T(8,128)(2,1)S(1)} %collective-permute-done.4.rest_3_), channel_id=1, source_target_pairs={{0,24},{24,48},{48,72},{72,96},{96,120},{120,144},{144,168},{168,0... | collective-permute-start | bytes 393224 | tf_op jit(solution)/shard_map/ppermute | solution.py:82
  55.0 4.0 %collective-permute-start.7 = (bf16[128,512]{1,0:T(8,128)(2,1)S(1)}, bf16[128,512]{1,0:T(8,128)(2,1)S(1)}, u32[]{:S(2)}, u32[]{:S(2)}) collective-permute-start(bf16[128,512]{1,0:T(8,128)(2,1)S(1)} %collective-permute-done.5.rest_4_), channel_id=1, source_target_pairs={{0,168},{24,0},{48,24},{72,48},{96,72},{120,96},{144,120},{168,144... | collective-permute-start | bytes 393224 | tf_op jit(solution)/shard_map/ppermute | solution.py:83
  58.9 1.0 collective-permute-done.6.rest_5_
  59.9 0.7 slice.8
  60.6 1.9 collective-permute-start.8
  63.4 4.9 %collective-permute-start.9 = (bf16[64,512]{1,0:T(8,128)(2,1)}, bf16[64,512]{1,0:T(8,128)(2,1)}, u32[]{:S(2)}, u32[]{:S(2)}) collective-permute-start(bf16[64,512]{1,0:T(8,128)(2,1)} %slice.9), channel_id=1, source_target_pairs={{0,168},{24,0},{48,24},{72,48},{96,72},{120,96},{144,120},{168,144... | collective-permute-start | bytes 196616 | tf_op jit(solution)/shard_map/ppermute | solution.py:87
  68.4 3.1 %collective-permute-done.9.rest_8_ = bf16[64,512]{1,0:T(8,128)(2,1)} collective-permute-done((bf16[64,512]{1,0:T(8,128)(2,1)}, bf16[64,512]{1,0:T(8,128)(2,1)}, u32[]{:S(2)}, u32[]{:S(2)}) %collective-permute-start.9) | collective-permute-done | bytes 65568 | tf_op jit(solution)/shard_map/ppermute | solution.py:87
  71.5 0.9 copy-done
  72.4 3.8 %local_term.1 = bf16[2112,128]{1,0:T(8,128)(2,1)} custom-call(s32[1]{0:T(128)} %bitcast.12.shard_ref, bf16[8,128,512]{2,1,0:T(8,128)(2,1)} %copy-done, bf16[128,512]{1,0:T(8,128)(2,1)} %get-tuple-element.10.rest_0_, bf16[128,512]{1,0:T(8,128)(2,1)} %copy-done.6, bf16[128,512]{1,0:T(8,128)(2,1)} %copy-done.7, bf16[128,512]{1,0:T(8,128)(2,1)} %copy-done.8, ...), custom_call_target="tpu_custom_call" | custom-call | tf_op jit(solution)/shard_map/local_term/pallas_call | solution.py:95
  76.2 40.9 %all_to_all.15.got_ref = bf16[24,88,128]{2,1,0:T(8,128)(2,1)} all-to-all(bf16[24,88,128]{2,1,0:T(8,128)(2,1)} %bitcast.26), channel_id=1, replica_groups=mesh['section'=4,'shard'=8,'replica'=24] {'replica'}, dimensions={0} | all-to-all | bytes 1081344 | tf_op jit(solution)/shard_map/all_to_all | solution.py:205
  117.1 1.9 sum_pieces.1
  119.1 6.2 %all-to-all-start.2 = ((bf16[24,88,128]{2,1,0:T(8,128)(2,1)}), bf16[24,88,128]{2,1,0:T(8,128)(2,1)S(1)}, u32[]{:S(2)}, u32[]{:S(2)}) async-start(bf16[24,88,128]{2,1,0:T(8,128)(2,1)} %sum_pieces.1), calls=%async_computation.2 | async-start | bytes 1081344 | tf_op jit(solution)/shard_map/all_to_all | solution.py:207
  125.2 2.3 collective-permute-start
  127.5 1.3 collective-permute-start.1
  129.5 0.7 dynamic-slice_multiply_fusion
  130.2 18.8 %all-to-all-done.2 = bf16[24,88,128]{2,1,0:T(8,128)(2,1)S(1)} async-done(((bf16[24,88,128]{2,1,0:T(8,128)(2,1)}), bf16[24,88,128]{2,1,0:T(8,128)(2,1)S(1)}, u32[]{:S(2)}, u32[]{:S(2)}) %all-to-all-start.2) | async-done | bytes 540704 | tf_op jit(solution)/shard_map/all_to_all | solution.py:207
  149.0 0.9 broadcast_in_dim.39.scale_ref
  149.9 2.2 spread.1
  152.1 73.8 %all-gather.2.cloned.1.call-done = bf16[4608,512]{1,0:T(8,128)(2,1)} async-done(((bf16[24,512]{1,0:T(8,128)(2,1)}), bf16[4608,512]{1,0:T(8,128)(2,1)}) %all-gather.2.cloned.1.call-update) | async-done | bytes 4718608 | tf_op jit(solution)/shard_map/all_gather | solution.py:199
  225.9 10.8 %window.1 = (bf16[128,512]{1,0:T(8,128)(2,1)}, bf16[128,4096]{1,0:T(8,128)(2,1)}) custom-call(bf16[8,576,512]{2,1,0:T(8,128)(2,1)} %bitcast.23, bf16[128,4096]{1,0:T(8,128)(2,1)} %bitcast.27, bf16[128,4096]{1,0:T(8,128)(2,1)} %collective-permute-done.came_fwd_ref, bf16[128,4096]{1,0:T(8,128)(2,1)} %bitcast.22, bf16[128,4096]{1,0:T(8,128)(2,1)} %bitcast.29, ...), custom_call_target="tpu_custom_call" | custom-call | tf_op jit(solution)/shard_map/window/pallas_call | solution.py:167
  (37 shorter events, 2.2 us)
Async XLA Ops:
  7.2 17.5 %copy-start.10 = (s32[1,128]{1,0:T(1,128)S(1)}, s32[1,128]{1,0:T(1,128)}, u32[]{:S(2)}) copy-start(s32[1,128]{1,0:T(1,128)} %param.9) | copy-start | bytes 1540
  7.2 17.5 %copy-start.11 = (s32[1,128]{1,0:T(1,128)S(1)}, s32[1,128]{1,0:T(1,128)}, u32[]{:S(2)}) copy-start(s32[1,128]{1,0:T(1,128)} %param.11) | copy-start | bytes 1540
  7.2 218.7 %all-gather.2.cloned.1.call-start = ((), (), s32[]{:S(2)}) async-start(), calls=%async_computation.3 | async-start | bytes 4743168 | tf_op jit(solution)/shard_map/all_gather | solution.py:199
  11.6 113.7 %copy-start.2 = (bf16[1,128,4096]{2,1,0:T(8,128)(2,1)S(1)}, bf16[1,128,4096]{2,1,0:T(8,128)(2,1)}, u32[]{:S(2)}) copy-start(bf16[1,128,4096]{2,1,0:T(8,128)(2,1)} %param.8) | copy-start | bytes 3145732
  11.6 116.0 %copy-start.3 = (bf16[1,128,4096]{2,1,0:T(8,128)(2,1)S(1)}, bf16[1,128,4096]{2,1,0:T(8,128)(2,1)}, u32[]{:S(2)}) copy-start(bf16[1,128,4096]{2,1,0:T(8,128)(2,1)} %param.12) | copy-start | bytes 3145732
  11.6 59.9 %all-to-all-start = ((bf16[8,128,512]{2,1,0:T(8,128)(2,1)}), bf16[8,128,512]{2,1,0:T(8,128)(2,1)S(1)}, u32[]{:S(2)}, u32[]{:S(2)}) async-start(bf16[8,128,512]{2,1,0:T(8,128)(2,1)} %bitcast.14), calls=%async_computation | async-start | bytes 2097152 | tf_op jit(solution)/shard_map/all_to_all | solution.py:192
  28.2 15.7 %collective-permute-start.2 = (bf16[128,512]{1,0:T(8,128)(2,1)}, bf16[128,512]{1,0:T(8,128)(2,1)S(1)}, u32[]{:S(2)}, u32[]{:S(2)}) collective-permute-start(bf16[128,512]{1,0:T(8,128)(2,1)} %get-tuple-element.10.rest_0_), channel_id=1, source_target_pairs={{0,24},{24,48},{48,72},{72,96},{96,120},{120,144},{144,168},{168,0... | collective-permute-start | bytes 393224 | tf_op jit(solution)/shard_map/ppermute | solution.py:82
  31.6 16.1 %collective-permute-start.3 = (bf16[128,512]{1,0:T(8,128)(2,1)}, bf16[128,512]{1,0:T(8,128)(2,1)S(1)}, u32[]{:S(2)}, u32[]{:S(2)}) collective-permute-start(bf16[128,512]{1,0:T(8,128)(2,1)} %get-tuple-element.10.rest_0_), channel_id=1, source_target_pairs={{0,168},{24,0},{48,24},{72,48},{96,72},{120,96},{144,120},{168,144... | collective-permute-start | bytes 393224 | tf_op jit(solution)/shard_map/ppermute | solution.py:83
  43.9 27.6 %copy-start.6 = (bf16[128,512]{1,0:T(8,128)(2,1)}, bf16[128,512]{1,0:T(8,128)(2,1)S(1)}, u32[]{:S(2)}) copy-start(bf16[128,512]{1,0:T(8,128)(2,1)S(1)} %collective-permute-done.2.rest_1_) | copy-start | bytes 393220
  43.9 7.9 %collective-permute-start.4 = (bf16[128,512]{1,0:T(8,128)(2,1)S(1)}, bf16[128,512]{1,0:T(8,128)(2,1)S(1)}, u32[]{:S(2)}, u32[]{:S(2)}) collective-permute-start(bf16[128,512]{1,0:T(8,128)(2,1)S(1)} %collective-permute-done.2.rest_1_), channel_id=1, source_target_pairs={{0,24},{24,48},{48,72},{72,96},{96,120},{120,144},{144,168},{168,0... | collective-permute-start | bytes 393224 | tf_op jit(solution)/shard_map/ppermute | solution.py:82
  47.7 6.8 %copy-start.7 = (bf16[128,512]{1,0:T(8,128)(2,1)}, bf16[128,512]{1,0:T(8,128)(2,1)S(1)}, u32[]{:S(2)}) copy-start(bf16[128,512]{1,0:T(8,128)(2,1)S(1)} %collective-permute-done.3.rest_2_) | copy-start | bytes 393220
  47.7 7.3 %collective-permute-start.5 = (bf16[128,512]{1,0:T(8,128)(2,1)S(1)}, bf16[128,512]{1,0:T(8,128)(2,1)S(1)}, u32[]{:S(2)}, u32[]{:S(2)}) collective-permute-start(bf16[128,512]{1,0:T(8,128)(2,1)S(1)} %collective-permute-done.3.rest_2_), channel_id=1, source_target_pairs={{0,168},{24,0},{48,24},{72,48},{96,72},{120,96},{144,120},{168,144... | collective-permute-start | bytes 393224 | tf_op jit(solution)/shard_map/ppermute | solution.py:83
  51.8 3.1 %copy-start.8 = (bf16[128,512]{1,0:T(8,128)(2,1)}, bf16[128,512]{1,0:T(8,128)(2,1)S(1)}, u32[]{:S(2)}) copy-start(bf16[128,512]{1,0:T(8,128)(2,1)S(1)} %collective-permute-done.4.rest_3_) | copy-start | bytes 393220
  51.8 8.1 %collective-permute-start.6 = (bf16[128,512]{1,0:T(8,128)(2,1)S(1)}, bf16[128,512]{1,0:T(8,128)(2,1)S(1)}, u32[]{:S(2)}, u32[]{:S(2)}) collective-permute-start(bf16[128,512]{1,0:T(8,128)(2,1)S(1)} %collective-permute-done.4.rest_3_), channel_id=1, source_target_pairs={{0,24},{24,48},{48,72},{72,96},{96,120},{120,144},{144,168},{168,0... | collective-permute-start | bytes 393224 | tf_op jit(solution)/shard_map/ppermute | solution.py:82
  55.0 7.8 %copy-start.9 = (bf16[128,512]{1,0:T(8,128)(2,1)}, bf16[128,512]{1,0:T(8,128)(2,1)S(1)}, u32[]{:S(2)}) copy-start(bf16[128,512]{1,0:T(8,128)(2,1)S(1)} %collective-permute-done.5.rest_4_) | copy-start | bytes 393220
  55.0 7.8 %collective-permute-start.7 = (bf16[128,512]{1,0:T(8,128)(2,1)S(1)}, bf16[128,512]{1,0:T(8,128)(2,1)S(1)}, u32[]{:S(2)}, u32[]{:S(2)}) collective-permute-start(bf16[128,512]{1,0:T(8,128)(2,1)S(1)} %collective-permute-done.5.rest_4_), channel_id=1, source_target_pairs={{0,168},{24,0},{48,24},{72,48},{96,72},{120,96},{144,120},{168,144... | collective-permute-start | bytes 393224 | tf_op jit(solution)/shard_map/ppermute | solution.py:83
  59.9 11.5 %copy-start.4 = (bf16[128,512]{1,0:T(8,128)(2,1)}, bf16[128,512]{1,0:T(8,128)(2,1)S(1)}, u32[]{:S(2)}) copy-start(bf16[128,512]{1,0:T(8,128)(2,1)S(1)} %collective-permute-done.6.rest_5_) | copy-start | bytes 393220
  60.6 7.8 %collective-permute-start.8 = (bf16[64,512]{1,0:T(8,128)(2,1)}, bf16[64,512]{1,0:T(8,128)(2,1)}, u32[]{:S(2)}, u32[]{:S(2)}) collective-permute-start(bf16[64,512]{1,0:T(8,128)(2,1)} %slice.8), channel_id=1, source_target_pairs={{0,24},{24,48},{48,72},{72,96},{96,120},{120,144},{144,168},{168,0... | collective-permute-start | bytes 196616 | tf_op jit(solution)/shard_map/ppermute | solution.py:86
  62.7 8.7 %copy-start.5 = (bf16[128,512]{1,0:T(8,128)(2,1)}, bf16[128,512]{1,0:T(8,128)(2,1)S(1)}, u32[]{:S(2)}) copy-start(bf16[128,512]{1,0:T(8,128)(2,1)S(1)} %collective-permute-done.7.rest_6_) | copy-start | bytes 393220
  63.4 8.0 %collective-permute-start.9 = (bf16[64,512]{1,0:T(8,128)(2,1)}, bf16[64,512]{1,0:T(8,128)(2,1)}, u32[]{:S(2)}, u32[]{:S(2)}) collective-permute-start(bf16[64,512]{1,0:T(8,128)(2,1)} %slice.9), channel_id=1, source_target_pairs={{0,168},{24,0},{48,24},{72,48},{96,72},{120,96},{144,120},{168,144... | collective-permute-start | bytes 196616 | tf_op jit(solution)/shard_map/ppermute | solution.py:87
  71.5 1.0 copy-start
  119.1 29.9 %all-to-all-start.2 = ((bf16[24,88,128]{2,1,0:T(8,128)(2,1)}), bf16[24,88,128]{2,1,0:T(8,128)(2,1)S(1)}, u32[]{:S(2)}, u32[]{:S(2)}) async-start(bf16[24,88,128]{2,1,0:T(8,128)(2,1)} %sum_pieces.1), calls=%async_computation.2 | async-start | bytes 1081344 | tf_op jit(solution)/shard_map/all_to_all | solution.py:207
  125.2 26.9 %collective-permute-start = (bf16[128,4096]{1,0:T(8,128)(2,1)S(1)}, bf16[128,4096]{1,0:T(8,128)(2,1)}, u32[]{:S(2)}, u32[]{:S(2)}) collective-permute-start(bf16[128,4096]{1,0:T(8,128)(2,1)S(1)} %bitcast.28), channel_id=1, source_target_pairs={{0,192},{192,384},{384,576},{1,193},{193,385},{385,577},{2,194},{1... | collective-permute-start | bytes 3145736 | tf_op jit(solution)/shard_map/ppermute | solution.py:19
  127.5 24.6 %collective-permute-start.1 = (bf16[128,4096]{1,0:T(8,128)(2,1)S(1)}, bf16[128,4096]{1,0:T(8,128)(2,1)}, u32[]{:S(2)}, u32[]{:S(2)}) collective-permute-start(bf16[128,4096]{1,0:T(8,128)(2,1)S(1)} %bitcast.30), channel_id=1, source_target_pairs={{192,0},{384,192},{576,384},{193,1},{385,193},{577,385},{194,2},{3... | collective-permute-start | bytes 3145736 | tf_op jit(solution)/shard_map/ppermute | solution.py:19
  149.0 0.9 copy-start.1
Sparse Core Ops, SparseCore 0:
  13.5 212.3 all-gather.1

commit v3 on v2

--- a/solution.py
+++ b/solution.py
@@ -30,6 +30,23 @@
 
 def turn(head, cosine, sine_part):
     return head * cosine + pltpu.roll(head, HEAD // 2, 1) * sine_part
+
+
+def pieces_kernel(rows_ref, out_ref):
+    out_ref[...] = rows_ref[...]
+
+
+def column_pieces(rows, count):
+    tokens, width = rows.shape
+    each = width // count
+    return pl.pallas_call(
+        pieces_kernel,
+        grid=(count,),
+        in_specs=[pl.BlockSpec((tokens, each), lambda i: (0, i))],
+        out_specs=pl.BlockSpec((None, tokens, each), lambda i: (i, 0, 0)),
+        out_shape=jax.ShapeDtypeStruct((count, tokens, each), rows.dtype),
+        name="column_pieces",
+    )(rows)
 
 
 def keys_kernel(saved_ref, cotan_ref, cos_ref, sin_ref, grad_ref, scaled_ref):
@@ -50,20 +67,20 @@
 
 
 def term_kernel(shard_ref, saved_ref, *rest):
-    *key_refs, out_ref, acc_ref = rest
-    count = saved_ref.shape[0]
+    *key_refs, out_ref, all_keys_ref = rest
+    count, tokens, rows = saved_ref.shape
+    cols = all_keys_ref.shape[1]
     for place, key_ref in enumerate(key_refs):
         distance, first = RING[place]
         block = lax.rem(shard_ref[0] + count - distance, count)
-        part = saved_ref[block, pl.ds(first, key_ref.shape[0]), :]
-        term = lax.dot_general(part, key_ref[...], (((0,), (0,)), ((), ())), preferred_element_type=F32)
-        if place == 0:
-            acc_ref[...] = term
-        else:
-            acc_ref[...] += term
-    rows, cols = acc_ref.shape
+        start = pl.multiple_of(block * tokens + first, HEAD // 2)
+        all_keys_ref[pl.ds(start, key_ref.shape[0]), :] = key_ref[...]
+    term = lax.dot_general(
+        saved_ref[...].reshape(count * tokens, rows), all_keys_ref[...], (((0,), (0,)), ((), ())),
+        preferred_element_type=F32,
+    )
     for block in range(cols // LANES):
-        out_ref[pl.ds(block * rows, rows), :] = acc_ref[:, pl.ds(block * LANES, LANES)].astype(BF16)
+        out_ref[pl.ds(block * rows, rows), :] = term[:, block * LANES : (block + 1) * LANES].astype(BF16)
     used = rows * cols // LANES
     if used < out_ref.shape[0]:
         out_ref[pl.ds(used, out_ref.shape[0] - used), :] = jnp.zeros((out_ref.shape[0] - used, LANES), BF16)
@@ -89,7 +106,6 @@
 
 
 def local_term(saved_cols, keys, shard, tall):
-    rows = saved_cols.shape[2]
     cols = keys[0].shape[1]
     vmem = pl.BlockSpec(memory_space=pltpu.VMEM)
     return pl.pallas_call(
@@ -97,18 +113,14 @@
         in_specs=[pl.BlockSpec(memory_space=pltpu.SMEM)] + [vmem] * (1 + len(keys)),
         out_specs=vmem,
         out_shape=jax.ShapeDtypeStruct((tall, LANES), BF16),
-        scratch_shapes=[pltpu.VMEM((rows, cols), F32)],
+        scratch_shapes=[pltpu.VMEM((saved_cols.shape[0] * saved_cols.shape[1], cols), BF16)],
         name="local_term",
     )(shard, saved_cols, *keys)
 
 
-def sum_kernel(got_ref, out_ref):
-    total = jnp.sum(got_ref[...].astype(F32), 0).astype(BF16)
-    out_ref[...] = jnp.broadcast_to(total[None], out_ref.shape)
-
-
 def sum_pieces(got):
-    return pl.pallas_call(sum_kernel, out_shape=jax.ShapeDtypeStruct(got.shape, BF16), name="sum_pieces")(got)
+    total = jnp.sum(got.astype(F32), 0).astype(BF16)
+    return jnp.broadcast_to(total[None], got.shape)
 
 
 def spread_kernel(full_ref, scale_ref, out_ref):
@@ -188,16 +200,12 @@
     _, tok_rows, _ = saved_acts.shape
     own_rows, cols = weight.shape[1:]
     gain_row = gain[0]
-    pieces = saved_acts[0].reshape(tok_rows, shard_count, own_rows).transpose(1, 0, 2)
+    pieces = column_pieces(saved_acts[0], shard_count)
     saved_cols = lax.all_to_all(pieces, "shard", split_axis=0, concat_axis=0)
     cos_b, sin_b = rope_tables(pos_bwd[0])
     key_grad, own_keys = key_factors(saved_acts[0], key_cotan[0], cos_b, sin_b)
     ring_keys = ring_blocks(own_keys)
-    share = -(-own_rows // (replica_count * 8)) * 8
-    padded = jnp.pad(weight[0], ((0, share * replica_count - own_rows), (0, 0)))
-    mine = lax.dynamic_slice(padded, (lax.axis_index("replica") * share, 0), (share, cols))
-    gathered = lax.all_gather(mine, ("shard", "replica"), axis=0, tiled=True)
-    gathered = gathered.reshape(shard_count, share * replica_count, cols)
+    gathered = lax.all_gather(weight[0], "shard", axis=0, tiled=True).reshape(shard_count, own_rows, cols)
     total = own_rows * cols // LANES
     piece = -(-total // (replica_count * 8)) * 8
     shard = lax.axis_index("shard").astype(jnp.int32)[None]

time: 244 us -> 192 us (0.79)
  the two profiles are of different devices: /device:TPU:8 before, /device:TPU:24 now
where the time goes in v3:
time: 192 us; the launch traced here: 191 us
  waiting for transfers between devices  56.7 us (30%)
  starting transfers between devices  48.2 us (25%)
  blocking collectives  41.1 us (21%)
  Pallas kernels  23.7 us (12%)
  between operations  14.3 us (7%)
  local copies, waits for them, and re-layouts  4.11 us (2%)
  other arithmetic  2.71 us (1%)
    all_to_all x1, blocking collectives, per_device(): lax.all_to_all(tall.reshape(replica_count, piece, LANES), 'replica', spli...  41.1 us
    ppermute x3, waiting for transfers between devices, ring_blocks(): came_right = lax.ppermute(came_right, 'shard', right)  32.3 us
    all_to_all x1, waiting for transfers between devices, per_device(): lax.all_to_all(own, 'replica', split_axis=0, concat_axis=0)  17.7 us
    all_to_all x1, starting transfers between devices, per_device(): saved_cols = lax.all_to_all(pieces, 'shard', split_axis=0, concat_axis=0)  12.7 us
    ppermute x3, starting transfers between devices, ring_blocks(): came_right = lax.ppermute(came_right, 'shard', right)  11.6 us
    pallas_call x1, Pallas kernels, window(): pl.pallas_call(window_kernel, grid=(width // block,), in_specs=[pl.BlockS...  10.8 us
    ppermute x3, starting transfers between devices, ring_blocks(): came_left = lax.ppermute(came_left, 'shard', left)  6.85 us
    all_to_all x1, starting transfers between devices, per_device(): lax.all_to_all(own, 'replica', split_axis=0, concat_axis=0)  5.87 us
  transfers between devices with their start and end apart: 13, of which 6 were waited for; matrix products, arithmetic and copies ran while one was open for 3% of the time, Pallas kernels for 7%

profile of v3, /device:TPU:24, one launch (start us, length us, event | category | flops | bytes accessed | tf_op | source)
XLA Modules:
  0.0 190.7 jit_solution(15336575614451414244)
XLA Ops:
  7.2 0.7 all-gather.3.cloned.1.call-update
  7.9 5.2 %column_pieces.1 = bf16[8,128,512]{2,1,0:T(8,128)(2,1)} custom-call(bf16[128,4096]{1,0:T(8,128)(2,1)} %bitcast.18), custom_call_target="tpu_custom_call" | custom-call | tf_op jit(solution)/shard_map/column_pieces/pallas_call | solution.py:42
  13.1 12.7 %all-to-all-start = ((bf16[8,128,512]{2,1,0:T(8,128)(2,1)}), bf16[8,128,512]{2,1,0:T(8,128)(2,1)S(1)}, u32[]{:S(2)}, u32[]{:S(2)}) async-start(bf16[8,128,512]{2,1,0:T(8,128)(2,1)} %column_pieces.1), calls=%async_computation | async-start | bytes 2097152 | tf_op jit(solution)/shard_map/all_to_all | solution.py:204
  25.9 1.2 fusion.1
  27.1 2.3 %key_factors.1 = (bf16[128,512]{1,0:T(8,128)(2,1)}, bf16[128,512]{1,0:T(8,128)(2,1)}) custom-call(bf16[128,4096]{1,0:T(8,128)(2,1)} %bitcast.19, bf16[128,512]{1,0:T(8,128)(2,1)} %bitcast.29, f32[128,128]{1,0:T(8,128)} %get-tuple-element.13.cos_ref, f32[128,128]{1,0:T(8,128)} %get-tuple-element.12.sin_ref), custom_call_target="tpu_custom_call" | custom-call | tf_op jit(solution)/shard_map/key_factors/pallas_call | solution.py:66
  29.4 4.6 %collective-permute-start.2 = (bf16[128,512]{1,0:T(8,128)(2,1)}, bf16[128,512]{1,0:T(8,128)(2,1)S(1)}, u32[]{:S(2)}, u32[]{:S(2)}) collective-permute-start(bf16[128,512]{1,0:T(8,128)(2,1)} %get-tuple-element.10.rest_0_), channel_id=1, source_target_pairs={{0,24},{24,48},{48,72},{72,96},{96,120},{120,144},{144,168},{168,0... | collective-permute-start | bytes 393224 | tf_op jit(solution)/shard_map/ppermute | solution.py:99
  34.0 1.9 %collective-permute-start.3 = (bf16[128,512]{1,0:T(8,128)(2,1)}, bf16[128,512]{1,0:T(8,128)(2,1)S(1)}, u32[]{:S(2)}, u32[]{:S(2)}) collective-permute-start(bf16[128,512]{1,0:T(8,128)(2,1)} %get-tuple-element.10.rest_0_), channel_id=1, source_target_pairs={{0,168},{24,0},{48,24},{72,48},{96,72},{120,96},{144,120},{168,144... | collective-permute-start | bytes 393224 | tf_op jit(solution)/shard_map/ppermute | solution.py:100
  35.9 23.2 %collective-permute-done.2.rest_1_ = bf16[128,512]{1,0:T(8,128)(2,1)S(1)} collective-permute-done((bf16[128,512]{1,0:T(8,128)(2,1)}, bf16[128,512]{1,0:T(8,128)(2,1)S(1)}, u32[]{:S(2)}, u32[]{:S(2)}) %collective-permute-start.2) | collective-permute-done | bytes 131104 | tf_op jit(solution)/shard_map/ppermute | solution.py:99
  59.1 2.8 %collective-permute-start.4 = (bf16[128,512]{1,0:T(8,128)(2,1)S(1)}, bf16[128,512]{1,0:T(8,128)(2,1)S(1)}, u32[]{:S(2)}, u32[]{:S(2)}) collective-permute-start(bf16[128,512]{1,0:T(8,128)(2,1)S(1)} %collective-permute-done.2.rest_1_), channel_id=1, source_target_pairs={{0,24},{24,48},{48,72},{72,96},{96,120},{120,144},{144,168},{168,0... | collective-permute-start | bytes 393224 | tf_op jit(solution)/shard_map/ppermute | solution.py:99
  61.9 3.0 %collective-permute-start.5 = (bf16[128,512]{1,0:T(8,128)(2,1)S(1)}, bf16[128,512]{1,0:T(8,128)(2,1)S(1)}, u32[]{:S(2)}, u32[]{:S(2)}) collective-permute-start(bf16[128,512]{1,0:T(8,128)(2,1)S(1)} %collective-permute-done.3.rest_2_), channel_id=1, source_target_pairs={{0,168},{24,0},{48,24},{72,48},{96,72},{120,96},{144,120},{168,144... | collective-permute-start | bytes 393224 | tf_op jit(solution)/shard_map/ppermute | solution.py:100
  64.9 5.0 %collective-permute-done.4.rest_3_ = bf16[128,512]{1,0:T(8,128)(2,1)S(1)} collective-permute-done((bf16[128,512]{1,0:T(8,128)(2,1)S(1)}, bf16[128,512]{1,0:T(8,128)(2,1)S(1)}, u32[]{:S(2)}, u32[]{:S(2)}) %collective-permute-start.4) | collective-permute-done | bytes 131104 | tf_op jit(solution)/shard_map/ppermute | solution.py:99
  70.0 4.2 %collective-permute-start.6 = (bf16[128,512]{1,0:T(8,128)(2,1)S(1)}, bf16[128,512]{1,0:T(8,128)(2,1)S(1)}, u32[]{:S(2)}, u32[]{:S(2)}) collective-permute-start(bf16[128,512]{1,0:T(8,128)(2,1)S(1)} %collective-permute-done.4.rest_3_), channel_id=1, source_target_pairs={{0,24},{24,48},{48,72},{72,96},{96,120},{120,144},{144,168},{168,0... | collective-permute-start | bytes 393224 | tf_op jit(solution)/shard_map/ppermute | solution.py:99
  74.3 1.9 %collective-permute-start.7 = (bf16[128,512]{1,0:T(8,128)(2,1)S(1)}, bf16[128,512]{1,0:T(8,128)(2,1)S(1)}, u32[]{:S(2)}, u32[]{:S(2)}) collective-permute-start(bf16[128,512]{1,0:T(8,128)(2,1)S(1)} %collective-permute-done.5.rest_4_), channel_id=1, source_target_pairs={{0,168},{24,0},{48,24},{72,48},{96,72},{120,96},{144,120},{168,144... | collective-permute-start | bytes 393224 | tf_op jit(solution)/shard_map/ppermute | solution.py:100
  76.2 4.1 %collective-permute-done.6.rest_5_ = bf16[128,512]{1,0:T(8,128)(2,1)S(1)} collective-permute-done((bf16[128,512]{1,0:T(8,128)(2,1)S(1)}, bf16[128,512]{1,0:T(8,128)(2,1)S(1)}, u32[]{:S(2)}, u32[]{:S(2)}) %collective-permute-start.6) | collective-permute-done | bytes 131104 | tf_op jit(solution)/shard_map/ppermute | solution.py:99
  80.3 0.7 slice.8
  81.0 5.6 %collective-permute-start.8 = (bf16[64,512]{1,0:T(8,128)(2,1)}, bf16[64,512]{1,0:T(8,128)(2,1)}, u32[]{:S(2)}, u32[]{:S(2)}) collective-permute-start(bf16[64,512]{1,0:T(8,128)(2,1)} %slice.8), channel_id=1, source_target_pairs={{0,24},{24,48},{48,72},{72,96},{96,120},{120,144},{144,168},{168,0... | collective-permute-start | bytes 196616 | tf_op jit(solution)/shard_map/ppermute | solution.py:103
  86.6 0.7 slice.9
  87.3 1.9 %collective-permute-start.9 = (bf16[64,512]{1,0:T(8,128)(2,1)}, bf16[64,512]{1,0:T(8,128)(2,1)}, u32[]{:S(2)}, u32[]{:S(2)}) collective-permute-start(bf16[64,512]{1,0:T(8,128)(2,1)} %slice.9), channel_id=1, source_target_pairs={{0,168},{24,0},{48,24},{72,48},{96,72},{120,96},{144,120},{168,144... | collective-permute-start | bytes 196616 | tf_op jit(solution)/shard_map/ppermute | solution.py:104
  89.2 1.0 collective-permute-done.8.rest_7_
  90.2 4.9 %collective-permute-done.9.rest_8_ = bf16[64,512]{1,0:T(8,128)(2,1)} collective-permute-done((bf16[64,512]{1,0:T(8,128)(2,1)}, bf16[64,512]{1,0:T(8,128)(2,1)}, u32[]{:S(2)}, u32[]{:S(2)}) %collective-permute-start.9) | collective-permute-done | bytes 65568 | tf_op jit(solution)/shard_map/ppermute | solution.py:104
  95.2 0.9 copy-done
  96.1 3.2 %local_term.1 = bf16[2112,128]{1,0:T(8,128)(2,1)} custom-call(s32[1]{0:T(128)} %bitcast.11.shard_ref, bf16[8,128,512]{2,1,0:T(8,128)(2,1)} %copy-done, bf16[128,512]{1,0:T(8,128)(2,1)} %get-tuple-element.10.rest_0_, bf16[128,512]{1,0:T(8,128)(2,1)} %copy-done.6, bf16[128,512]{1,0:T(8,128)(2,1)} %copy-done.7, bf16[128,512]{1,0:T(8,128)(2,1)} %copy-done.8, ...), custom_call_target="tpu_custom_call" | custom-call | tf_op jit(solution)/shard_map/local_term/pallas_call | solution.py:111
  99.3 41.1 %all_to_all.15 = bf16[24,88,128]{2,1,0:T(8,128)(2,1)S(1)} all-to-all(bf16[24,88,128]{2,1,0:T(8,128)(2,1)} %bitcast.23), channel_id=1, replica_groups=mesh['section'=4,'shard'=8,'replica'=24] {'replica'}, dimensions={0} | all-to-all | bytes 1081344 | tf_op jit(solution)/shard_map/all_to_all | solution.py:213
  140.4 0.9 broadcast_in_dim.45
  141.3 5.9 %all-to-all-start.2 = ((bf16[24,88,128]{2,1,0:T(8,128)(2,1)}), bf16[24,88,128]{2,1,0:T(8,128)(2,1)S(1)}, u32[]{:S(2)}, u32[]{:S(2)}) async-start(bf16[24,88,128]{2,1,0:T(8,128)(2,1)} %broadcast_in_dim.45), calls=%async_computation.2 | async-start | bytes 1081344 | tf_op jit(solution)/shard_map/all_to_all | solution.py:215
  147.2 2.3 %collective-permute-start = (bf16[128,4096]{1,0:T(8,128)(2,1)S(1)}, bf16[128,4096]{1,0:T(8,128)(2,1)}, u32[]{:S(2)}, u32[]{:S(2)}) collective-permute-start(bf16[128,4096]{1,0:T(8,128)(2,1)S(1)} %bitcast.25), channel_id=1, source_target_pairs={{0,192},{192,384},{384,576},{1,193},{193,385},{385,577},{2,194},{1... | collective-permute-start | bytes 3145736 | tf_op jit(solution)/shard_map/ppermute | solution.py:19
  149.5 1.3 collective-permute-start.1
  151.5 0.7 dynamic-slice_multiply_fusion
  152.2 17.7 %all-to-all-done.2 = bf16[24,88,128]{2,1,0:T(8,128)(2,1)S(1)} async-done(((bf16[24,88,128]{2,1,0:T(8,128)(2,1)}), bf16[24,88,128]{2,1,0:T(8,128)(2,1)S(1)}, u32[]{:S(2)}, u32[]{:S(2)}) %all-to-all-start.2) | async-done | bytes 540704 | tf_op jit(solution)/shard_map/all_to_all | solution.py:215
  169.9 0.9 broadcast_in_dim.46.scale_ref
  170.8 2.2 %spread.1 = f32[512,512]{1,0:T(8,128)} custom-call(bf16[2112,128]{1,0:T(8,128)(2,1)} %bitcast.22, f32[512,128]{1,0:T(8,128)} %broadcast_in_dim.46.scale_ref), custom_call_target="tpu_custom_call" | custom-call | tf_op jit(solution)/shard_map/spread/pallas_call | solution.py:134
  173.1 10.8 %window.1 = (bf16[128,512]{1,0:T(8,128)(2,1)}, bf16[128,4096]{1,0:T(8,128)(2,1)}) custom-call(bf16[8,512,512]{2,1,0:T(8,128)(2,1)} %bitcast.21, bf16[128,4096]{1,0:T(8,128)(2,1)} %bitcast.24, bf16[128,4096]{1,0:T(8,128)(2,1)} %collective-permute-done.came_fwd_ref, bf16[128,4096]{1,0:T(8,128)(2,1)} %bitcast.20, bf16[128,4096]{1,0:T(8,128)(2,1)} %bitcast.26, ...), custom_call_target="tpu_custom_call" | custom-call | tf_op jit(solution)/shard_map/window/pallas_call | solution.py:179
  (36 shorter events, 1.0 us)
Async XLA Ops:
  7.2 18.7 %copy-start.10 = (s32[1,128]{1,0:T(1,128)S(1)}, s32[1,128]{1,0:T(1,128)}, u32[]{:S(2)}) copy-start(s32[1,128]{1,0:T(1,128)} %param.9) | copy-start | bytes 1540
  7.2 18.7 %copy-start.11 = (s32[1,128]{1,0:T(1,128)S(1)}, s32[1,128]{1,0:T(1,128)}, u32[]{:S(2)}) copy-start(s32[1,128]{1,0:T(1,128)} %param.11) | copy-start | bytes 1540
  7.2 165.9 %all-gather.3.cloned.1.call-start = ((), (), s32[]{:S(2)}) async-start(), calls=%async_computation.3 | async-start | bytes 4718592 | tf_op jit(solution)/shard_map/all_gather | solution.py:208
  13.1 82.1 %all-to-all-start = ((bf16[8,128,512]{2,1,0:T(8,128)(2,1)}), bf16[8,128,512]{2,1,0:T(8,128)(2,1)S(1)}, u32[]{:S(2)}, u32[]{:S(2)}) async-start(bf16[8,128,512]{2,1,0:T(8,128)(2,1)} %column_pieces.1), calls=%async_computation | async-start | bytes 2097152 | tf_op jit(solution)/shard_map/all_to_all | solution.py:204
  25.8 121.4 %copy-start.2 = (bf16[1,128,4096]{2,1,0:T(8,128)(2,1)S(1)}, bf16[1,128,4096]{2,1,0:T(8,128)(2,1)}, u32[]{:S(2)}) copy-start(bf16[1,128,4096]{2,1,0:T(8,128)(2,1)} %param.8) | copy-start | bytes 3145732
  25.8 123.7 %copy-start.3 = (bf16[1,128,4096]{2,1,0:T(8,128)(2,1)S(1)}, bf16[1,128,4096]{2,1,0:T(8,128)(2,1)}, u32[]{:S(2)}) copy-start(bf16[1,128,4096]{2,1,0:T(8,128)(2,1)} %param.12) | copy-start | bytes 3145732
  29.4 29.7 %collective-permute-start.2 = (bf16[128,512]{1,0:T(8,128)(2,1)}, bf16[128,512]{1,0:T(8,128)(2,1)S(1)}, u32[]{:S(2)}, u32[]{:S(2)}) collective-permute-start(bf16[128,512]{1,0:T(8,128)(2,1)} %get-tuple-element.10.rest_0_), channel_id=1, source_target_pairs={{0,24},{24,48},{48,72},{72,96},{96,120},{120,144},{144,168},{168,0... | collective-permute-start | bytes 393224 | tf_op jit(solution)/shard_map/ppermute | solution.py:99
  34.0 27.9 %collective-permute-start.3 = (bf16[128,512]{1,0:T(8,128)(2,1)}, bf16[128,512]{1,0:T(8,128)(2,1)S(1)}, u32[]{:S(2)}, u32[]{:S(2)}) collective-permute-start(bf16[128,512]{1,0:T(8,128)(2,1)} %get-tuple-element.10.rest_0_), channel_id=1, source_target_pairs={{0,168},{24,0},{48,24},{72,48},{96,72},{120,96},{144,120},{168,144... | collective-permute-start | bytes 393224 | tf_op jit(solution)/shard_map/ppermute | solution.py:100
  59.1 36.1 %copy-start.6 = (bf16[128,512]{1,0:T(8,128)(2,1)}, bf16[128,512]{1,0:T(8,128)(2,1)S(1)}, u32[]{:S(2)}) copy-start(bf16[128,512]{1,0:T(8,128)(2,1)S(1)} %collective-permute-done.2.rest_1_) | copy-start | bytes 393220
  59.1 10.9 %collective-permute-start.4 = (bf16[128,512]{1,0:T(8,128)(2,1)S(1)}, bf16[128,512]{1,0:T(8,128)(2,1)S(1)}, u32[]{:S(2)}, u32[]{:S(2)}) collective-permute-start(bf16[128,512]{1,0:T(8,128)(2,1)S(1)} %collective-permute-done.2.rest_1_), channel_id=1, source_target_pairs={{0,24},{24,48},{48,72},{72,96},{96,120},{120,144},{144,168},{168,0... | collective-permute-start | bytes 393224 | tf_op jit(solution)/shard_map/ppermute | solution.py:99
  61.9 12.3 %copy-start.7 = (bf16[128,512]{1,0:T(8,128)(2,1)}, bf16[128,512]{1,0:T(8,128)(2,1)S(1)}, u32[]{:S(2)}) copy-start(bf16[128,512]{1,0:T(8,128)(2,1)S(1)} %collective-permute-done.3.rest_2_) | copy-start | bytes 393220
  61.9 12.3 %collective-permute-start.5 = (bf16[128,512]{1,0:T(8,128)(2,1)S(1)}, bf16[128,512]{1,0:T(8,128)(2,1)S(1)}, u32[]{:S(2)}, u32[]{:S(2)}) collective-permute-start(bf16[128,512]{1,0:T(8,128)(2,1)S(1)} %collective-permute-done.3.rest_2_), channel_id=1, source_target_pairs={{0,168},{24,0},{48,24},{72,48},{96,72},{120,96},{144,120},{168,144... | collective-permute-start | bytes 393224 | tf_op jit(solution)/shard_map/ppermute | solution.py:100
  70.0 4.3 %copy-start.8 = (bf16[128,512]{1,0:T(8,128)(2,1)}, bf16[128,512]{1,0:T(8,128)(2,1)S(1)}, u32[]{:S(2)}) copy-start(bf16[128,512]{1,0:T(8,128)(2,1)S(1)} %collective-permute-done.4.rest_3_) | copy-start | bytes 393220
  70.0 10.3 %collective-permute-start.6 = (bf16[128,512]{1,0:T(8,128)(2,1)S(1)}, bf16[128,512]{1,0:T(8,128)(2,1)S(1)}, u32[]{:S(2)}, u32[]{:S(2)}) collective-permute-start(bf16[128,512]{1,0:T(8,128)(2,1)S(1)} %collective-permute-done.4.rest_3_), channel_id=1, source_target_pairs={{0,24},{24,48},{48,72},{72,96},{96,120},{120,144},{144,168},{168,0... | collective-permute-start | bytes 393224 | tf_op jit(solution)/shard_map/ppermute | solution.py:99
  74.3 12.4 %copy-start.9 = (bf16[128,512]{1,0:T(8,128)(2,1)}, bf16[128,512]{1,0:T(8,128)(2,1)S(1)}, u32[]{:S(2)}) copy-start(bf16[128,512]{1,0:T(8,128)(2,1)S(1)} %collective-permute-done.5.rest_4_) | copy-start | bytes 393220
  74.3 12.3 %collective-permute-start.7 = (bf16[128,512]{1,0:T(8,128)(2,1)S(1)}, bf16[128,512]{1,0:T(8,128)(2,1)S(1)}, u32[]{:S(2)}, u32[]{:S(2)}) collective-permute-start(bf16[128,512]{1,0:T(8,128)(2,1)S(1)} %collective-permute-done.5.rest_4_), channel_id=1, source_target_pairs={{0,168},{24,0},{48,24},{72,48},{96,72},{120,96},{144,120},{168,144... | collective-permute-start | bytes 393224 | tf_op jit(solution)/shard_map/ppermute | solution.py:100
  80.3 14.8 %copy-start.4 = (bf16[128,512]{1,0:T(8,128)(2,1)}, bf16[128,512]{1,0:T(8,128)(2,1)S(1)}, u32[]{:S(2)}) copy-start(bf16[128,512]{1,0:T(8,128)(2,1)S(1)} %collective-permute-done.6.rest_5_) | copy-start | bytes 393220
  81.0 9.2 %collective-permute-start.8 = (bf16[64,512]{1,0:T(8,128)(2,1)}, bf16[64,512]{1,0:T(8,128)(2,1)}, u32[]{:S(2)}, u32[]{:S(2)}) collective-permute-start(bf16[64,512]{1,0:T(8,128)(2,1)} %slice.8), channel_id=1, source_target_pairs={{0,24},{24,48},{48,72},{72,96},{96,120},{120,144},{144,168},{168,0... | collective-permute-start | bytes 196616 | tf_op jit(solution)/shard_map/ppermute | solution.py:103
  86.6 8.6 %copy-start.5 = (bf16[128,512]{1,0:T(8,128)(2,1)}, bf16[128,512]{1,0:T(8,128)(2,1)S(1)}, u32[]{:S(2)}) copy-start(bf16[128,512]{1,0:T(8,128)(2,1)S(1)} %collective-permute-done.7.rest_6_) | copy-start | bytes 393220
  87.3 7.8 %collective-permute-start.9 = (bf16[64,512]{1,0:T(8,128)(2,1)}, bf16[64,512]{1,0:T(8,128)(2,1)}, u32[]{:S(2)}, u32[]{:S(2)}) collective-permute-start(bf16[64,512]{1,0:T(8,128)(2,1)} %slice.9), channel_id=1, source_target_pairs={{0,168},{24,0},{48,24},{72,48},{96,72},{120,96},{144,120},{168,144... | collective-permute-start | bytes 196616 | tf_op jit(solution)/shard_map/ppermute | solution.py:104
  95.1 1.0 copy-start
  141.3 28.6 %all-to-all-start.2 = ((bf16[24,88,128]{2,1,0:T(8,128)(2,1)}), bf16[24,88,128]{2,1,0:T(8,128)(2,1)S(1)}, u32[]{:S(2)}, u32[]{:S(2)}) async-start(bf16[24,88,128]{2,1,0:T(8,128)(2,1)} %broadcast_in_dim.45), calls=%async_computation.2 | async-start | bytes 1081344 | tf_op jit(solution)/shard_map/all_to_all | solution.py:215
  147.2 25.8 %collective-permute-start = (bf16[128,4096]{1,0:T(8,128)(2,1)S(1)}, bf16[128,4096]{1,0:T(8,128)(2,1)}, u32[]{:S(2)}, u32[]{:S(2)}) collective-permute-start(bf16[128,4096]{1,0:T(8,128)(2,1)S(1)} %bitcast.25), channel_id=1, source_target_pairs={{0,192},{192,384},{384,576},{1,193},{193,385},{385,577},{2,194},{1... | collective-permute-start | bytes 3145736 | tf_op jit(solution)/shard_map/ppermute | solution.py:19
  149.5 23.5 %collective-permute-start.1 = (bf16[128,4096]{1,0:T(8,128)(2,1)S(1)}, bf16[128,4096]{1,0:T(8,128)(2,1)}, u32[]{:S(2)}, u32[]{:S(2)}) collective-permute-start(bf16[128,4096]{1,0:T(8,128)(2,1)S(1)} %bitcast.27), channel_id=1, source_target_pairs={{192,0},{384,192},{576,384},{193,1},{385,193},{577,385},{194,2},{3... | collective-permute-start | bytes 3145736 | tf_op jit(solution)/shard_map/ppermute | solution.py:19
  169.9 0.9 copy-start.1
Sparse Core Ops, SparseCore 0:
  10.4 84.4 all-gather.2

commit v4 on v2

--- a/solution.py
+++ b/solution.py
@@ -49,77 +49,21 @@
     return pl.pallas_call(keys_kernel, out_shape=(shape, shape), name="key_factors")(saved, cotan, cosine, sine_part)
 
 
-def term_kernel(shard_ref, saved_ref, *rest):
-    *key_refs, out_ref, acc_ref = rest
-    count = saved_ref.shape[0]
-    for place, key_ref in enumerate(key_refs):
-        distance, first = RING[place]
-        block = lax.rem(shard_ref[0] + count - distance, count)
-        part = saved_ref[block, pl.ds(first, key_ref.shape[0]), :]
-        term = lax.dot_general(part, key_ref[...], (((0,), (0,)), ((), ())), preferred_element_type=F32)
-        if place == 0:
-            acc_ref[...] = term
-        else:
-            acc_ref[...] += term
-    rows, cols = acc_ref.shape
-    for block in range(cols // LANES):
-        out_ref[pl.ds(block * rows, rows), :] = acc_ref[:, pl.ds(block * LANES, LANES)].astype(BF16)
-    used = rows * cols // LANES
-    if used < out_ref.shape[0]:
-        out_ref[pl.ds(used, out_ref.shape[0] - used), :] = jnp.zeros((out_ref.shape[0] - used, LANES), BF16)
-
-
-RING = ((0, 0), (1, 0), (7, 0), (2, 0), (6, 0), (3, 0), (5, 0), (4, 0), (4, 64))
-
-
-def ring_blocks(rows):
-    count = lax.axis_size("shard")
-    right = [(i, (i + 1) % count) for i in range(count)]
-    left = [(i, (i - 1) % count) for i in range(count)]
-    blocks = [rows]
-    came_right = came_left = rows
-    for _ in range(count // 2 - 1):
-        came_right = lax.ppermute(came_right, "shard", right)
-        came_left = lax.ppermute(came_left, "shard", left)
-        blocks += [came_right, came_left]
-    half = rows.shape[0] // 2
-    blocks.append(lax.ppermute(came_right[:half], "shard", right))
-    blocks.append(lax.ppermute(came_left[half:], "shard", left))
-    return blocks
-
-
-def local_term(saved_cols, keys, shard, tall):
-    rows = saved_cols.shape[2]
-    cols = keys[0].shape[1]
-    vmem = pl.BlockSpec(memory_space=pltpu.VMEM)
-    return pl.pallas_call(
-        term_kernel,
-        in_specs=[pl.BlockSpec(memory_space=pltpu.SMEM)] + [vmem] * (1 + len(keys)),
-        out_specs=vmem,
-        out_shape=jax.ShapeDtypeStruct((tall, LANES), BF16),
-        scratch_shapes=[pltpu.VMEM((rows, cols), F32)],
-        name="local_term",
-    )(shard, saved_cols, *keys)
-
-
-def sum_kernel(got_ref, out_ref):
-    total = jnp.sum(got_ref[...].astype(F32), 0).astype(BF16)
-    out_ref[...] = jnp.broadcast_to(total[None], out_ref.shape)
+def tall_pieces(term, count):
+    rows, cols = term.shape
+    tall = term.astype(BF16).reshape(rows, cols // LANES, LANES).transpose(1, 0, 2).reshape(-1, LANES)
+    piece = -(-tall.shape[0] // (count * 8)) * 8
+    return jnp.pad(tall, ((0, piece * count - tall.shape[0]), (0, 0))).reshape(count, piece, LANES)
 
 
 def sum_pieces(got):
-    return pl.pallas_call(sum_kernel, out_shape=jax.ShapeDtypeStruct(got.shape, BF16), name="sum_pieces")(got)
+    total = jnp.sum(got.astype(F32), 0).astype(BF16)
+    return jnp.broadcast_to(total[None], got.shape)
 
 
-def spread_kernel(full_ref, scale_ref, out_ref):
-    rows, cols = out_ref.shape
-    scale = scale_ref[...]
-    for block in range(cols // LANES):
-        out_ref[:, pl.ds(block * LANES, LANES)] = full_ref[pl.ds(block * rows, rows), :].astype(F32) * scale
-
-
-def spread(full, scale, rows, cols):
-    return pl.pallas_call(spread_kernel, out_shape=jax.ShapeDtypeStruct((rows, cols), F32), name="spread")(full, scale)
+def from_tall(full, rows, cols):
+    full = full.reshape(-1, LANES)[: rows * cols // LANES].astype(F32)
+    return full.reshape(cols // LANES, rows, LANES).transpose(1, 0, 2).reshape(rows, cols)
 
 
 def window_kernel(
@@ -190,25 +134,19 @@
     gain_row = gain[0]
     pieces = saved_acts[0].reshape(tok_rows, shard_count, own_rows).transpose(1, 0, 2)
     saved_cols = lax.all_to_all(pieces, "shard", split_axis=0, concat_axis=0)
+    saved_cols = saved_cols.reshape(shard_count * tok_rows, own_rows)
     cos_b, sin_b = rope_tables(pos_bwd[0])
     key_grad, own_keys = key_factors(saved_acts[0], key_cotan[0], cos_b, sin_b)
-    ring_keys = ring_blocks(own_keys)
-    share = -(-own_rows // (replica_count * 8)) * 8
-    padded = jnp.pad(weight[0], ((0, share * replica_count - own_rows), (0, 0)))
-    mine = lax.dynamic_slice(padded, (lax.axis_index("replica") * share, 0), (share, cols))
-    gathered = lax.all_gather(mine, ("shard", "replica"), axis=0, tiled=True)
-    gathered = gathered.reshape(shard_count, share * replica_count, cols)
-    total = own_rows * cols // LANES
-    piece = -(-total // (replica_count * 8)) * 8
-    shard = lax.axis_index("shard").astype(jnp.int32)[None]
-    tall = local_term(saved_cols, ring_keys, shard, piece * replica_count)
-    got = lax.all_to_all(tall.reshape(replica_count, piece, LANES), "replica", split_axis=0, concat_axis=0)
+    scaled_keys = lax.all_gather(own_keys, "shard", axis=0, tiled=True)
+    gathered = lax.all_gather(weight[0], "shard", axis=0, tiled=True).reshape(shard_count, own_rows, cols)
+    term = lax.dot_general(saved_cols, scaled_keys, (((0,), (0,)), ((), ())), preferred_element_type=F32)
+    got = lax.all_to_all(tall_pieces(term, replica_count), "replica", split_axis=0, concat_axis=0)
     own = sum_pieces(got)
-    full = lax.all_to_all(own, "replica", split_axis=0, concat_axis=0).reshape(-1, LANES)
+    full = lax.all_to_all(own, "replica", split_axis=0, concat_axis=0)
     token_total = tok_rows * shard_count * replica_count
     own_gain = lax.dynamic_slice(gain_row, (lax.axis_index("shard") * own_rows,), (own_rows,))
-    scale = jnp.broadcast_to((own_gain * float(token_total) ** (-0.5))[:, None], (own_rows, LANES))
-    weight_grad = spread(full, scale, own_rows, cols)
+    scale = own_gain * float(token_total) ** (-0.5)
+    weight_grad = from_tall(full, own_rows, cols) * scale[:, None]
     came_fwd = from_behind(acts_fwd[0], "section", 1)
     came_bwd = from_behind(grads_in[0], "section", -1)
     cos_f, sin_f = rope_tables(pos_fwd[0])

time: 244 us -> 155 us (0.64)
  the two profiles are of different devices: /device:TPU:8 before, /device:TPU:4 now
where the time goes in v4:
time: 155 us; the launch traced here: 154 us
  blocking collectives  77.8 us (50%)
  waiting for transfers between devices  28.3 us (18%)
  between operations  14.1 us (9%)
  Pallas kernels  13.1 us (8%)
  starting transfers between devices  10 us (6%)
  local copies, waits for them, and re-layouts  4.99 us (3%)
  other arithmetic  3.56 us (2%)
  matrix products  2.04 us (1%)
    all_to_all x1, blocking collectives, per_device(): saved_cols = lax.all_to_all(pieces, 'shard', split_axis=0, concat_axis=0)  39.7 us
    all_to_all x1, blocking collectives, per_device(): lax.all_to_all(tall_pieces(term, replica_count), 'replica', split_axis=0,...  38 us
    all_to_all x1, waiting for transfers between devices, per_device(): full = lax.all_to_all(own, 'replica', split_axis=0, concat_axis=0)  16.6 us
    all_gather x1, waiting for transfers between devices, per_device(): scaled_keys = lax.all_gather(own_keys, 'shard', axis=0, tiled=True)  11 us
    pallas_call x1, Pallas kernels, window(): pl.pallas_call(window_kernel, grid=(width // block,), in_specs=[pl.BlockS...  10.8 us
    all_to_all x1, starting transfers between devices, per_device(): full = lax.all_to_all(own, 'replica', split_axis=0, concat_axis=0)  6.42 us
    ppermute x2, starting transfers between devices, from_behind(): return lax.ppermute(x, axis, pairs)  3.54 us
  transfers between devices with their start and end apart: 5, of which 2 were waited for; matrix products, arithmetic and copies ran while one was open for 6% of the time, Pallas kernels for 0%

profile of v4, /device:TPU:4, one launch (start us, length us, event | category | flops | bytes accessed | tf_op | source)
XLA Modules:
  0.0 154.0 jit_solution(15968153728082625912)
XLA Ops:
  7.2 0.0 all-gather.4.cloned.1.call-start
  7.2 0.1 compare_select_fusion
  7.3 0.7 convert_bitcast_fusion.1
  8.0 1.2 fusion.1
  9.2 2.3 %key_factors.1 = (bf16[128,512]{1,0:T(8,128)(2,1)}, bf16[128,512]{1,0:T(8,128)(2,1)}) custom-call(bf16[128,4096]{1,0:T(8,128)(2,1)} %bitcast.34, bf16[128,512]{1,0:T(8,128)(2,1)} %bitcast.46, f32[128,128]{1,0:T(8,128)} %get-tuple-element.16.cos_ref, f32[128,128]{1,0:T(8,128)} %get-tuple-element.15.sin_ref), custom_call_target="tpu_custom_call" | custom-call | tf_op jit(solution)/shard_map/key_factors/pallas_call | solution.py:49
  11.5 0.0 all-gather.4.cloned.1.call-update
  11.5 0.0 all-gather.6.cloned.1.call-start
  11.6 0.7 all-gather.6.cloned.1.call-update
  12.3 1.6 %copy.12 = bf16[1,128,4096]{1,2,0:T(8,128)(2,1)S(1)} copy(bf16[1,128,4096]{2,1,0:T(8,128)(2,1)} %param.10) | data formatting | bytes 2097152 | tf_op args[2]
  13.9 39.7 %all_to_all.15 = bf16[8,128,512]{1,2,0:T(8,128)(2,1)S(1)} all-to-all(bf16[8,128,512]{1,2,0:T(8,128)(2,1)S(1)} %bitcast.37), channel_id=1, replica_groups=mesh['section'=4,'shard'=8,'replica'=24] {'shard'}, dimensions={0} | all-to-all | bytes 2097152 | tf_op jit(solution)/shard_map/all_to_all | solution.py:136
  53.6 0.5 copy.13
  54.2 11.0 %all-gather.4.cloned.1.call-done = bf16[1024,512]{1,0:T(8,128)(2,1)} async-done(((bf16[128,512]{1,0:T(8,128)(2,1)}), bf16[1024,512]{1,0:T(8,128)(2,1)}) %all-gather.4.cloned.1.call-update) | async-done | bytes 1048592 | tf_op jit(solution)/shard_map/all_gather | solution.py:140
  65.2 0.0 copy-start
  65.2 2.0 %convolution_convert_fusion = bf16[512,512]{1,0:T(8,128)(2,1)S(1)} fusion(bf16[1024,512]{1,0:T(8,128)(2,1)} %all-gather.4.cloned.1.call-done, bf16[1024,512]{1,0:T(8,128)(2,1)S(1)} %bitcast.44), kind=kOutput, calls=%fused_computation | convolution fusion | flops 537133056 | bytes 2621440 | tf_op jit(solution)/shard_map/dot_general | solution.py:142
  67.2 0.3 copy.14
  67.5 38.0 %all_to_all.16 = bf16[24,88,128]{2,1,0:T(8,128)(2,1)S(1)} all-to-all(bf16[24,88,128]{2,1,0:T(8,128)(2,1)S(1)} %bitcast.38), channel_id=1, replica_groups=mesh['section'=4,'shard'=8,'replica'=24] {'replica'}, dimensions={0} | all-to-all | bytes 1081344 | tf_op jit(solution)/shard_map/all_to_all | solution.py:143
  105.6 0.1 reduce_sum.12
  105.6 0.9 broadcast_in_dim.34
  106.5 6.4 %all-to-all-start.2 = ((bf16[24,88,128]{2,1,0:T(8,128)(2,1)}), bf16[24,88,128]{2,1,0:T(8,128)(2,1)S(1)}, u32[]{:S(2)}, u32[]{:S(2)}) async-start(bf16[24,88,128]{2,1,0:T(8,128)(2,1)} %broadcast_in_dim.34), calls=%async_computation.2 | async-start | bytes 1081344 | tf_op jit(solution)/shard_map/all_to_all | solution.py:145
  112.9 0.0 copy-done
  113.0 2.3 %collective-permute-start = (bf16[128,4096]{1,0:T(8,128)(2,1)S(1)}, bf16[128,4096]{1,0:T(8,128)(2,1)}, u32[]{:S(2)}, u32[]{:S(2)}) collective-permute-start(bf16[128,4096]{1,0:T(8,128)(2,1)S(1)} %bitcast.43), channel_id=1, source_target_pairs={{0,192},{192,384},{384,576},{1,193},{193,385},{385,577},{2,194},{1... | collective-permute-start | bytes 3145736 | tf_op jit(solution)/shard_map/ppermute | solution.py:19
  115.2 1.3 collective-permute-start.1
  116.5 0.6 pad_add_fusion.place_ref
  117.1 0.7 dynamic-slice_multiply_fusion
  117.8 16.6 %all-to-all-done.2 = bf16[24,88,128]{2,1,0:T(8,128)(2,1)S(1)} async-done(((bf16[24,88,128]{2,1,0:T(8,128)(2,1)}), bf16[24,88,128]{2,1,0:T(8,128)(2,1)S(1)}, u32[]{:S(2)}, u32[]{:S(2)}) %all-to-all-start.2) | async-done | bytes 540704 | tf_op jit(solution)/shard_map/all_to_all | solution.py:145
  134.5 0.1 convert_bitcast_fusion
  134.6 0.3 copy.15
  134.9 0.1 bitcast_multiply_fusion
  135.1 1.3 copy.16
  136.4 0.0 collective-permute-done.came_fwd_ref
  136.4 0.0 collective-permute-done.1.came_bwd_ref
  136.4 10.8 %window.1 = (bf16[128,512]{1,0:T(8,128)(2,1)}, bf16[128,4096]{1,0:T(8,128)(2,1)}) custom-call(bf16[8,512,512]{2,1,0:T(8,128)(2,1)} %bitcast.36, bf16[128,4096]{1,0:T(8,128)(2,1)} %bitcast.42, bf16[128,4096]{1,0:T(8,128)(2,1)} %collective-permute-done.came_fwd_ref, bf16[128,4096]{1,0:T(8,128)(2,1)} %bitcast.35, bf16[128,4096]{1,0:T(8,128)(2,1)} %bitcast.3.grads_ref, ...), custom_call_target="tpu_custom_call" | custom-call | tf_op jit(solution)/shard_map/window/pallas_call | solution.py:111
  (4 shorter events, 0.1 us)
Async XLA Ops:
  7.2 58.0 %all-gather.4.cloned.1.call-start = ((), (), s32[]{:S(2)}) async-start(), calls=%async_computation.3 | async-start | bytes 1179648 | tf_op jit(solution)/shard_map/all_gather | solution.py:140
  11.5 124.9 %all-gather.6.cloned.1.call-start = ((), (), s32[]{:S(2)}) async-start(), calls=%async_computation.4 | async-start | bytes 4718592 | tf_op jit(solution)/shard_map/all_gather | solution.py:141
  65.2 47.8 %copy-start = (bf16[1,128,4096]{2,1,0:T(8,128)(2,1)S(1)}, bf16[1,128,4096]{2,1,0:T(8,128)(2,1)}, u32[]{:S(2)}) copy-start(bf16[1,128,4096]{2,1,0:T(8,128)(2,1)} %param.8) | copy-start | bytes 3145732
  106.5 27.9 %all-to-all-start.2 = ((bf16[24,88,128]{2,1,0:T(8,128)(2,1)}), bf16[24,88,128]{2,1,0:T(8,128)(2,1)S(1)}, u32[]{:S(2)}, u32[]{:S(2)}) async-start(bf16[24,88,128]{2,1,0:T(8,128)(2,1)} %broadcast_in_dim.34), calls=%async_computation.2 | async-start | bytes 1081344 | tf_op jit(solution)/shard_map/all_to_all | solution.py:145
  113.0 23.4 %collective-permute-start = (bf16[128,4096]{1,0:T(8,128)(2,1)S(1)}, bf16[128,4096]{1,0:T(8,128)(2,1)}, u32[]{:S(2)}, u32[]{:S(2)}) collective-permute-start(bf16[128,4096]{1,0:T(8,128)(2,1)S(1)} %bitcast.43), channel_id=1, source_target_pairs={{0,192},{192,384},{384,576},{1,193},{193,385},{385,577},{2,194},{1... | collective-permute-start | bytes 3145736 | tf_op jit(solution)/shard_map/ppermute | solution.py:19
  115.2 21.2 %collective-permute-start.1 = (bf16[128,4096]{1,0:T(8,128)(2,1)}, bf16[128,4096]{1,0:T(8,128)(2,1)}, u32[]{:S(2)}, u32[]{:S(2)}) collective-permute-start(bf16[128,4096]{1,0:T(8,128)(2,1)} %bitcast.3.grads_ref), channel_id=1, source_target_pairs={{192,0},{384,192},{576,384},{193,1},{385,193},{577,385},{194,2},{3... | collective-permute-start | bytes 3145736 | tf_op jit(solution)/shard_map/ppermute | solution.py:19
Sparse Core Ops, SparseCore 0:
  11.6 53.4 all-gather.3
  67.5 61.6 all-gather.5

commit v5 on v4

--- a/solution.py
+++ b/solution.py
@@ -66,62 +66,107 @@
     return full.reshape(cols // LANES, rows, LANES).transpose(1, 0, 2).reshape(rows, cols)
 
 
+def streams_kernel(acts_ref, came_fwd_ref, grads_ref, came_bwd_ref, saved_ref, gain_ref, place_ref, normed_ref, arrived_ref, inverse_ref):
+    stream = jnp.where(place_ref[0] == 0, acts_ref[...], came_fwd_ref[...]).astype(F32)
+    inverse = lax.rsqrt(jnp.mean(stream * stream, -1, keepdims=True) + EPS)
+    normed_ref[...] = (stream * inverse * gain_ref[...]).astype(BF16)
+    arrived_ref[...] = jnp.where(place_ref[1] == 0, grads_ref[...], came_bwd_ref[...])
+    saved = saved_ref[...].astype(F32)
+    inverse = lax.rsqrt(jnp.mean(saved * saved, -1, keepdims=True) + EPS)
+    inverse_ref[...] = jnp.broadcast_to(inverse, inverse_ref.shape)
+
+
+def streams(acts, came_fwd, grads, came_bwd, saved, gain_row, place):
+    tokens, width = acts.shape
+    group = 32
+    rows = pl.BlockSpec((group, width), lambda i: (i, 0))
+    return pl.pallas_call(
+        streams_kernel,
+        grid=(tokens // group,),
+        in_specs=[rows] * 5 + [pl.BlockSpec((1, width), lambda i: (0, 0)), pl.BlockSpec(memory_space=pltpu.SMEM)],
+        out_specs=(rows, rows, pl.BlockSpec((group, LANES), lambda i: (i, 0))),
+        out_shape=(
+            jax.ShapeDtypeStruct((tokens, width), BF16),
+            jax.ShapeDtypeStruct((tokens, width), BF16),
+            jax.ShapeDtypeStruct((tokens, LANES), F32),
+        ),
+        name="streams",
+    )(acts, came_fwd, grads, came_bwd, saved, gain_row, place)
+
+
 def window_kernel(
-    weight_ref, acts_ref, came_fwd_ref, saved_ref, grads_ref, came_bwd_ref, key_grad_ref, gain_ref, cos_ref, sin_ref,
-    place_ref, keys_ref, grad_out_ref, normed_ref, proj_ref, ng_ref,
+    weight_ref, normed_ref, saved_ref, arrived_ref, key_grad_ref, gain_ref, inverse_ref, cos_ref, sin_ref,
+    keys_ref, grad_out_ref, proj_ref, scaled_ref, pull_ref,
 ):
-    step = pl.program_id(0)
+    finish = pl.program_id(0)
+    step = pl.program_id(1)
     block = weight_ref.shape[0]
-    span = pl.ds(pl.multiple_of(step * block, block), block)
-
-    @pl.when(step == 0)
+    width = block * pl.num_programs(1)
+
+    @pl.when(finish == 0)
     def _():
-        stream = jnp.where(place_ref[0] == 0, acts_ref[...], came_fwd_ref[...]).astype(F32)
-        inverse = lax.rsqrt(jnp.mean(stream * stream, -1, keepdims=True) + EPS)
-        normed_ref[...] = (stream * inverse * gain_ref[...]).astype(BF16)
-        proj_ref[...] = jnp.zeros_like(proj_ref)
-
-    rows = weight_ref[...]
-    proj_ref[...] += jnp.dot(normed_ref[:, span], rows, preferred_element_type=F32)
-    ng_ref[:, span] = (
-        lax.dot_general(key_grad_ref[...], rows, (((1,), (1,)), ((), ())), preferred_element_type=F32)
-        * gain_ref[:, span]
-    )
-
-    @pl.when(step == pl.num_programs(0) - 1)
+        rows = weight_ref[...]
+        part = jnp.dot(normed_ref[...], rows, preferred_element_type=F32)
+        scaled = (
+            lax.dot_general(key_grad_ref[...], rows, (((1,), (1,)), ((), ())), preferred_element_type=F32)
+            * gain_ref[...]
+        )
+        scaled_ref[step] = scaled
+        pull = jnp.broadcast_to(jnp.sum(saved_ref[...].astype(F32) * scaled, -1, keepdims=True), pull_ref.shape)
+
+        @pl.when(step == 0)
+        def _():
+            proj_ref[...] = part
+            pull_ref[...] = pull
+
+        @pl.when(step > 0)
+        def _():
+            proj_ref[...] += part
+            pull_ref[...] += pull
+
+    @pl.when(finish == 1)
     def _():
-        cosine = cos_ref[...]
-        sine_part = sin_ref[...]
-        for start in range(0, keys_ref.shape[1], HEAD):
-            head = pl.ds(start, HEAD)
-            keys_ref[:, head] = turn(proj_ref[:, head], cosine, sine_part).astype(BF16)
-        saved = saved_ref[...].astype(F32)
-        inverse = lax.rsqrt(jnp.mean(saved * saved, -1, keepdims=True) + EPS)
-        scaled = ng_ref[...]
-        pull = inverse * inverse * inverse * jnp.mean(saved * scaled, -1, keepdims=True)
-        arrived = jnp.where(place_ref[1] == 0, grads_ref[...], came_bwd_ref[...]).astype(F32)
-        grad_out_ref[...] = (arrived + (inverse * scaled - saved * pull)).astype(BF16)
-
-
-def window(weight, acts, came_fwd, saved, grads, came_bwd, key_grad, gain_row, cosine, sine_part, place):
-    tokens, width = acts.shape
-    cols = weight.shape[2]
-    block = width // weight.shape[0]
-    whole = lambda *shape: pl.BlockSpec(shape, lambda i: (0,) * len(shape))
+        @pl.when(step == 0)
+        def _():
+            cosine = cos_ref[...]
+            sine_part = sin_ref[...]
+            for start in range(0, keys_ref.shape[1], HEAD):
+                head = pl.ds(start, HEAD)
+                keys_ref[:, head] = turn(proj_ref[:, head], cosine, sine_part).astype(BF16)
+
+        inverse = inverse_ref[:, :1]
+        pull = inverse * inverse * inverse * (pull_ref[:, :1] / width)
+        grad = inverse * scaled_ref[step] - saved_ref[...].astype(F32) * pull
+        grad_out_ref[...] = (arrived_ref[...].astype(F32) + grad).astype(BF16)
+
+
+def window(weight, normed, saved, arrived, key_grad, gain_row, inverse, cosine, sine_part):
+    tokens, width = normed.shape
+    cols = weight.shape[1]
+    steps = 4
+    block = width // steps
+    whole = lambda *shape: pl.BlockSpec(shape, lambda p, i: (0,) * len(shape))
+    first = lambda p, i: i + p * (steps - 1 - i)
+    last = lambda p, i: p * i
     return pl.pallas_call(
         window_kernel,
-        grid=(width // block,),
+        grid=(2, steps),
         in_specs=[
-            pl.BlockSpec((None, block, cols), lambda i: (i, 0, 0)),
-            whole(tokens, width), whole(tokens, width), whole(tokens, width), whole(tokens, width), whole(tokens, width),
-            whole(tokens, cols), whole(1, width), whole(tokens, HEAD), whole(tokens, HEAD),
-            pl.BlockSpec(memory_space=pltpu.SMEM),
+            pl.BlockSpec((block, cols), lambda p, i: (first(p, i), 0)),
+            pl.BlockSpec((tokens, block), lambda p, i: (0, first(p, i))),
+            pl.BlockSpec((tokens, block), lambda p, i: (0, i)),
+            pl.BlockSpec((tokens, block), lambda p, i: (0, last(p, i))),
+            whole(tokens, cols),
+            pl.BlockSpec((1, block), lambda p, i: (0, first(p, i))),
+            whole(tokens, LANES), whole(tokens, HEAD), whole(tokens, HEAD),
         ],
-        out_specs=(whole(tokens, cols), whole(tokens, width)),
+        out_specs=(whole(tokens, cols), pl.BlockSpec((tokens, block), lambda p, i: (0, last(p, i)))),
         out_shape=(jax.ShapeDtypeStruct((tokens, cols), BF16), jax.ShapeDtypeStruct((tokens, width), BF16)),
-        scratch_shapes=[pltpu.VMEM((tokens, width), BF16), pltpu.VMEM((tokens, cols), F32), pltpu.VMEM((tokens, width), F32)],
+        scratch_shapes=[
+            pltpu.VMEM((tokens, cols), F32), pltpu.VMEM((steps, tokens, block), F32), pltpu.VMEM((tokens, LANES), F32)
+        ],
         name="window",
-    )(weight, acts, came_fwd, saved, grads, came_bwd, key_grad, gain_row, cosine, sine_part, place)
+    )(weight, normed, saved, arrived, key_grad, gain_row, inverse, cosine, sine_part)
 
 
 def per_device(acts_fwd, pos_fwd, saved_acts, pos_bwd, grads_in, key_cotan, weight, gain):
@@ -138,7 +183,7 @@
     cos_b, sin_b = rope_tables(pos_bwd[0])
     key_grad, own_keys = key_factors(saved_acts[0], key_cotan[0], cos_b, sin_b)
     scaled_keys = lax.all_gather(own_keys, "shard", axis=0, tiled=True)
-    gathered = lax.all_gather(weight[0], "shard", axis=0, tiled=True).reshape(shard_count, own_rows, cols)
+    gathered = lax.all_gather(weight[0], "shard", axis=0, tiled=True)
     term = lax.dot_general(saved_cols, scaled_keys, (((0,), (0,)), ((), ())), preferred_element_type=F32)
     got = lax.all_to_all(tall_pieces(term, replica_count), "replica", split_axis=0, concat_axis=0)
     own = sum_pieces(got)
@@ -151,8 +196,11 @@
     came_bwd = from_behind(grads_in[0], "section", -1)
     cos_f, sin_f = rope_tables(pos_fwd[0])
     place = jnp.stack([section_pos, section_count - 1 - section_pos]).astype(jnp.int32)
+    normed, arrived, inverse = streams(
+        acts_fwd[0], came_fwd, grads_in[0], came_bwd, saved_acts[0], gain_row[None], place
+    )
     keys, grad_out = window(
-        gathered, acts_fwd[0], came_fwd, saved_acts[0], grads_in[0], came_bwd, key_grad, gain_row[None], cos_f, sin_f, place
+        gathered, normed, saved_acts[0], arrived, key_grad, gain_row[None], inverse, cos_f, sin_f
     )
     return (keys[None], grad_out[None], weight_grad[None])
 

time: 155 us -> 159 us (1.026)
  the two profiles are of different devices: /device:TPU:4 before, /device:TPU:5 now
where the time goes in v5:
time: 159 us
  blocking collectives  72.6 us (46%)
  waiting for transfers between devices  27.7 us (17%)
  starting transfers between devices  17.7 us (11%)
  Pallas kernels  15.8 us (10%)
  between operations  14.2 us (9%)
  local copies, waits for them, and re-layouts  5 us (3%)
  other arithmetic  3.54 us (2%)
  matrix products  2.04 us (1%)
    all_to_all x1, blocking collectives, per_device(): saved_cols = lax.all_to_all(pieces, 'shard', split_axis=0, concat_axis=0)  37.7 us
    all_to_all x1, blocking collectives, per_device(): lax.all_to_all(tall_pieces(term, replica_count), 'replica', split_axis=0,...  34.9 us
    ppermute x2, waiting for transfers between devices, from_behind(): return lax.ppermute(x, axis, pairs)  16.8 us
    all_gather x1, waiting for transfers between devices, per_device(): scaled_keys = lax.all_gather(own_keys, 'shard', axis=0, tiled=True)  10.1 us
    all_to_all x1, starting transfers between devices, per_device(): full = lax.all_to_all(own, 'replica', split_axis=0, concat_axis=0)  9.2 us
    pallas_call x1, Pallas kernels, window(): pl.pallas_call(window_kernel, grid=(2, steps), in_specs=[pl.BlockSpec((bl...  8.84 us
    ppermute x2, starting transfers between devices, from_behind(): return lax.ppermute(x, axis, pairs)  8.4 us
    pallas_call x1, Pallas kernels, streams(): pl.pallas_call(streams_kernel, grid=(tokens // group,), in_specs=[rows] *...  4.65 us
  transfers between devices with their start and end apart: 5, of which 3 were waited for; matrix products, arithmetic and copies ran while one was open for 5% of the time, Pallas kernels for 3%

profile of v5, /device:TPU:5, one launch (start us, length us, event | category | flops | bytes accessed | tf_op | source)
XLA Modules:
  0.0 158.5 jit_solution(2961296076608802790)
XLA Ops:
  7.2 0.0 all-gather.4.cloned.1.call-start
  7.2 0.1 compare_select_fusion
  7.3 0.7 convert_bitcast_fusion.1
  8.0 1.2 fusion.1
  9.2 2.3 %key_factors.1 = (bf16[128,512]{1,0:T(8,128)(2,1)}, bf16[128,512]{1,0:T(8,128)(2,1)}) custom-call(bf16[128,4096]{1,0:T(8,128)(2,1)} %bitcast.34, bf16[128,512]{1,0:T(8,128)(2,1)} %bitcast.49, f32[128,128]{1,0:T(8,128)} %get-tuple-element.22.cos_ref, f32[128,128]{1,0:T(8,128)} %get-tuple-element.21.sin_ref), custom_call_target="tpu_custom_call" | custom-call | tf_op jit(solution)/shard_map/key_factors/pallas_call | solution.py:49
  11.5 0.0 all-gather.4.cloned.1.call-update
  11.5 0.0 all-gather.6.cloned.1.call-start
  11.6 0.7 all-gather.6.cloned.1.call-update
  12.3 1.6 %copy.12 = bf16[1,128,4096]{1,2,0:T(8,128)(2,1)S(1)} copy(bf16[1,128,4096]{2,1,0:T(8,128)(2,1)} %param.10) | data formatting | bytes 2097152 | tf_op args[2]
  13.9 37.7 %all_to_all.15 = bf16[8,128,512]{1,2,0:T(8,128)(2,1)S(1)} all-to-all(bf16[8,128,512]{1,2,0:T(8,128)(2,1)S(1)} %bitcast.38), channel_id=1, replica_groups=mesh['section'=4,'shard'=8,'replica'=24] {'shard'}, dimensions={0} | all-to-all | bytes 2097152 | tf_op jit(solution)/shard_map/all_to_all | solution.py:181
  51.6 0.5 copy.13
  52.1 10.1 %all-gather.4.cloned.1.call-done = bf16[1024,512]{1,0:T(8,128)(2,1)} async-done(((bf16[128,512]{1,0:T(8,128)(2,1)}), bf16[1024,512]{1,0:T(8,128)(2,1)}) %all-gather.4.cloned.1.call-update) | async-done | bytes 1048592 | tf_op jit(solution)/shard_map/all_gather | solution.py:185
  62.3 2.0 %convolution_convert_fusion = bf16[512,512]{1,0:T(8,128)(2,1)S(1)} fusion(bf16[1024,512]{1,0:T(8,128)(2,1)} %all-gather.4.cloned.1.call-done, bf16[1024,512]{1,0:T(8,128)(2,1)S(1)} %bitcast.43), kind=kOutput, calls=%fused_computation | convolution fusion | flops 537133056 | bytes 2621440 | tf_op jit(solution)/shard_map/dot_general | solution.py:187
  64.3 0.0 copy-start.1
  64.3 0.3 copy.14
  64.7 34.9 %all_to_all.16 = bf16[24,88,128]{2,1,0:T(8,128)(2,1)S(1)} all-to-all(bf16[24,88,128]{2,1,0:T(8,128)(2,1)S(1)} %bitcast.39), channel_id=1, replica_groups=mesh['section'=4,'shard'=8,'replica'=24] {'replica'}, dimensions={0} | all-to-all | bytes 1081344 | tf_op jit(solution)/shard_map/all_to_all | solution.py:188
  99.5 0.1 reduce_sum.12
  99.6 0.9 broadcast_in_dim.34
  100.5 9.2 %all-to-all-start.2 = ((bf16[24,88,128]{2,1,0:T(8,128)(2,1)}), bf16[24,88,128]{2,1,0:T(8,128)(2,1)S(1)}, u32[]{:S(2)}, u32[]{:S(2)}) async-start(bf16[24,88,128]{2,1,0:T(8,128)(2,1)} %broadcast_in_dim.34), calls=%async_computation.2 | async-start | bytes 1081344 | tf_op jit(solution)/shard_map/all_to_all | solution.py:190
  109.7 6.5 %collective-permute-start = (bf16[128,4096]{1,0:T(8,128)(2,1)S(1)}, bf16[128,4096]{1,0:T(8,128)(2,1)}, u32[]{:S(2)}, u32[]{:S(2)}) collective-permute-start(bf16[128,4096]{1,0:T(8,128)(2,1)S(1)} %bitcast.45), channel_id=1, source_target_pairs={{0,192},{192,384},{384,576},{1,193},{193,385},{385,577},{2,194},{1... | collective-permute-start | bytes 3145736 | tf_op jit(solution)/shard_map/ppermute | solution.py:19
  116.2 1.9 %collective-permute-start.1 = (bf16[128,4096]{1,0:T(8,128)(2,1)S(1)}, bf16[128,4096]{1,0:T(8,128)(2,1)}, u32[]{:S(2)}, u32[]{:S(2)}) collective-permute-start(bf16[128,4096]{1,0:T(8,128)(2,1)S(1)} %bitcast.47), channel_id=1, source_target_pairs={{192,0},{384,192},{576,384},{193,1},{385,193},{577,385},{194,2},{3... | collective-permute-start | bytes 3145736 | tf_op jit(solution)/shard_map/ppermute | solution.py:19
  118.1 0.6 pad_add_fusion.place_ref
  118.7 0.7 dynamic-slice_multiply_fusion
  119.4 12.9 %collective-permute-done.came_fwd_ref = bf16[128,4096]{1,0:T(8,128)(2,1)} collective-permute-done((bf16[128,4096]{1,0:T(8,128)(2,1)S(1)}, bf16[128,4096]{1,0:T(8,128)(2,1)}, u32[]{:S(2)}, u32[]{:S(2)}) %collective-permute-start) | collective-permute-done | bytes 1048608 | tf_op jit(solution)/shard_map/ppermute | solution.py:19
  132.3 3.9 %collective-permute-done.1.came_bwd_ref = bf16[128,4096]{1,0:T(8,128)(2,1)} collective-permute-done((bf16[128,4096]{1,0:T(8,128)(2,1)S(1)}, bf16[128,4096]{1,0:T(8,128)(2,1)}, u32[]{:S(2)}, u32[]{:S(2)}) %collective-permute-start.1) | collective-permute-done | bytes 1048608 | tf_op jit(solution)/shard_map/ppermute | solution.py:19
  136.2 4.6 %streams.1 = (bf16[128,4096]{1,0:T(8,128)(2,1)}, bf16[128,4096]{1,0:T(8,128)(2,1)}, f32[128,128]{1,0:T(8,128)}) custom-call(bf16[128,4096]{1,0:T(8,128)(2,1)} %bitcast.44, bf16[128,4096]{1,0:T(8,128)(2,1)} %collective-permute-done.came_fwd_ref, bf16[128,4096]{1,0:T(8,128)(2,1)} %bitcast.46, bf16[128,4096]{1,0:T(8,128)(2,1)} %collective-permute-done.1.came_bwd_ref, ...), custom_call_target="tpu_custom_call" | custom-call | tf_op jit(solution)/shard_map/streams/pallas_call | solution.py:83
  140.9 0.0 all-to-all-done.2
  140.9 0.1 convert_bitcast_fusion
  141.0 0.3 copy.15
  141.4 0.1 bitcast_multiply_fusion
  141.5 1.3 copy.16
  142.8 8.8 %window.1 = (bf16[128,512]{1,0:T(8,128)(2,1)}, bf16[128,4096]{1,0:T(8,128)(2,1)}) custom-call(bf16[4096,512]{1,0:T(8,128)(2,1)} %bitcast.37, bf16[128,4096]{1,0:T(8,128)(2,1)} %get-tuple-element.10.normed_ref, bf16[128,4096]{1,0:T(8,128)(2,1)} %bitcast.36, bf16[128,4096]{1,0:T(8,128)(2,1)} %get-tuple-element.11.arrived_ref, ...), custom_call_target="tpu_custom_call" | custom-call | tf_op jit(solution)/shard_map/window/pallas_call | solution.py:151
  (7 shorter events, 0.1 us)
Async XLA Ops:
  7.2 55.1 %all-gather.4.cloned.1.call-start = ((), (), s32[]{:S(2)}) async-start(), calls=%async_computation.3 | async-start | bytes 1179648 | tf_op jit(solution)/shard_map/all_gather | solution.py:185
  11.5 131.3 %all-gather.6.cloned.1.call-start = ((), (), s32[]{:S(2)}) async-start(), calls=%async_computation.4 | async-start | bytes 4718592 | tf_op jit(solution)/shard_map/all_gather | solution.py:186
  62.3 47.4 %copy-start = (bf16[1,128,4096]{2,1,0:T(8,128)(2,1)S(1)}, bf16[1,128,4096]{2,1,0:T(8,128)(2,1)}, u32[]{:S(2)}) copy-start(bf16[1,128,4096]{2,1,0:T(8,128)(2,1)} %param.8) | copy-start | bytes 3145732
  64.3 51.9 %copy-start.1 = (bf16[1,128,4096]{2,1,0:T(8,128)(2,1)S(1)}, bf16[1,128,4096]{2,1,0:T(8,128)(2,1)}, u32[]{:S(2)}) copy-start(bf16[1,128,4096]{2,1,0:T(8,128)(2,1)} %param.12) | copy-start | bytes 3145732
  100.5 40.4 %all-to-all-start.2 = ((bf16[24,88,128]{2,1,0:T(8,128)(2,1)}), bf16[24,88,128]{2,1,0:T(8,128)(2,1)S(1)}, u32[]{:S(2)}, u32[]{:S(2)}) async-start(bf16[24,88,128]{2,1,0:T(8,128)(2,1)} %broadcast_in_dim.34), calls=%async_computation.2 | async-start | bytes 1081344 | tf_op jit(solution)/shard_map/all_to_all | solution.py:190
  109.7 22.6 %collective-permute-start = (bf16[128,4096]{1,0:T(8,128)(2,1)S(1)}, bf16[128,4096]{1,0:T(8,128)(2,1)}, u32[]{:S(2)}, u32[]{:S(2)}) collective-permute-start(bf16[128,4096]{1,0:T(8,128)(2,1)S(1)} %bitcast.45), channel_id=1, source_target_pairs={{0,192},{192,384},{384,576},{1,193},{193,385},{385,577},{2,194},{1... | collective-permute-start | bytes 3145736 | tf_op jit(solution)/shard_map/ppermute | solution.py:19
  116.2 20.1 %collective-permute-start.1 = (bf16[128,4096]{1,0:T(8,128)(2,1)S(1)}, bf16[128,4096]{1,0:T(8,128)(2,1)}, u32[]{:S(2)}, u32[]{:S(2)}) collective-permute-start(bf16[128,4096]{1,0:T(8,128)(2,1)S(1)} %bitcast.47), channel_id=1, source_target_pairs={{192,0},{384,192},{576,384},{193,1},{385,193},{577,385},{194,2},{3... | collective-permute-start | bytes 3145736 | tf_op jit(solution)/shard_map/ppermute | solution.py:19
Sparse Core Ops, SparseCore 0:
  11.6 50.5 all-gather.3
  64.6 64.3 all-gather.5

commit v6 on v5

--- a/solution.py
+++ b/solution.py
@@ -46,7 +46,16 @@
 
 def key_factors(saved, cotan, cosine, sine_part):
     shape = jax.ShapeDtypeStruct(cotan.shape, BF16)
-    return pl.pallas_call(keys_kernel, out_shape=(shape, shape), name="key_factors")(saved, cotan, cosine, sine_part)
+    group = 32
+    rows = lambda array: pl.BlockSpec((group, array.shape[1]), lambda i: (i, 0))
+    return pl.pallas_call(
+        keys_kernel,
+        grid=(cotan.shape[0] // group,),
+        in_specs=[rows(saved), rows(cotan), rows(cosine), rows(sine_part)],
+        out_specs=(rows(cotan), rows(cotan)),
+        out_shape=(shape, shape),
+        name="key_factors",
+    )(saved, cotan, cosine, sine_part)
 
 
 def tall_pieces(term, count):
@@ -194,7 +203,8 @@
     weight_grad = from_tall(full, own_rows, cols) * scale[:, None]
     came_fwd = from_behind(acts_fwd[0], "section", 1)
     came_bwd = from_behind(grads_in[0], "section", -1)
-    cos_f, sin_f = rope_tables(pos_fwd[0])
+    later, _ = lax.optimization_barrier((pos_fwd[0], key_grad))
+    cos_f, sin_f = rope_tables(later)
     place = jnp.stack([section_pos, section_count - 1 - section_pos]).astype(jnp.int32)
     normed, arrived, inverse = streams(
         acts_fwd[0], came_fwd, grads_in[0], came_bwd, saved_acts[0], gain_row[None], place

time: 159 us -> 160 us (level)
  transfers between devices with their start and end apart: 5 -> 5, of which waited for: 3 -> 3; matrix products, arithmetic and copies ran while one was open for 5% -> 6% of each run, Pallas kernels for 3% -> 3%
where the time goes in v6:
time: 160 us; the launch traced here: 159 us
  blocking collectives  72.5 us (45%)
  waiting for transfers between devices  26.7 us (17%)
  starting transfers between devices  17.7 us (11%)
  Pallas kernels  17 us (11%)
  between operations  14.2 us (9%)
  local copies, waits for them, and re-layouts  5.01 us (3%)
  other arithmetic  4.25 us (3%)
  matrix products  2.04 us (1%)
    all_to_all x1, blocking collectives, per_device(): saved_cols = lax.all_to_all(pieces, 'shard', split_axis=0, concat_axis=0)  37.7 us
    all_to_all x1, blocking collectives, per_device(): lax.all_to_all(tall_pieces(term, replica_count), 'replica', split_axis=0,...  34.8 us
    ppermute x2, waiting for transfers between devices, from_behind(): return lax.ppermute(x, axis, pairs)  15.9 us
    all_gather x1, waiting for transfers between devices, per_device(): scaled_keys = lax.all_gather(own_keys, 'shard', axis=0, tiled=True)  10.1 us
    all_to_all x1, starting transfers between devices, per_device(): full = lax.all_to_all(own, 'replica', split_axis=0, concat_axis=0)  9.26 us
    pallas_call x1, Pallas kernels, window(): pl.pallas_call(window_kernel, grid=(2, steps), in_specs=[pl.BlockSpec((bl...  8.84 us
    ppermute x2, starting transfers between devices, from_behind(): return lax.ppermute(x, axis, pairs)  8.41 us
    pallas_call x1, Pallas kernels, streams(): pl.pallas_call(streams_kernel, grid=(tokens // group,), in_specs=[rows] *...  4.64 us
  transfers between devices with their start and end apart: 5, of which 3 were waited for; matrix products, arithmetic and copies ran while one was open for 6% of the time, Pallas kernels for 3%

profile of v6, /device:TPU:5, one launch (start us, length us, event | category | flops | bytes accessed | tf_op | source)
XLA Modules:
  0.0 159.5 jit_solution(18301502087688839843)
XLA Ops:
  7.2 0.0 all-gather.4.cloned.1.call-start
  7.2 0.1 compare_select_fusion
  7.3 0.7 convert_bitcast_fusion.1
  8.0 1.0 fusion
  8.9 3.5 %key_factors.1 = (bf16[128,512]{1,0:T(8,128)(2,1)}, bf16[128,512]{1,0:T(8,128)(2,1)}) custom-call(bf16[128,4096]{1,0:T(8,128)(2,1)} %bitcast.33, bf16[128,512]{1,0:T(8,128)(2,1)} %bitcast.48, f32[128,128]{1,0:T(8,128)} %get-tuple-element.25.cos_ref, f32[128,128]{1,0:T(8,128)} %get-tuple-element.24.sin_ref), custom_call_target="tpu_custom_call" | custom-call | tf_op jit(solution)/shard_map/key_factors/pallas_call | solution.py:51
  12.5 0.0 all-gather.4.cloned.1.call-update
  12.5 0.0 all-gather.6.cloned.1.call-start
  12.5 0.7 all-gather.6.cloned.1.call-update
  13.2 1.6 %copy.12 = bf16[1,128,4096]{1,2,0:T(8,128)(2,1)S(1)} copy(bf16[1,128,4096]{2,1,0:T(8,128)(2,1)} %param.10) | data formatting | bytes 2097152 | tf_op args[2]
  14.9 37.7 %all_to_all.15 = bf16[8,128,512]{1,2,0:T(8,128)(2,1)S(1)} all-to-all(bf16[8,128,512]{1,2,0:T(8,128)(2,1)S(1)} %bitcast.37), channel_id=1, replica_groups=mesh['section'=4,'shard'=8,'replica'=24] {'shard'}, dimensions={0} | all-to-all | bytes 2097152 | tf_op jit(solution)/shard_map/all_to_all | solution.py:190
  52.6 0.5 copy.13
  53.1 10.1 %all-gather.4.cloned.1.call-done = bf16[1024,512]{1,0:T(8,128)(2,1)} async-done(((bf16[128,512]{1,0:T(8,128)(2,1)}), bf16[1024,512]{1,0:T(8,128)(2,1)}) %all-gather.4.cloned.1.call-update) | async-done | bytes 1048592 | tf_op jit(solution)/shard_map/all_gather | solution.py:194
  63.2 2.0 %convolution_convert_fusion = bf16[512,512]{1,0:T(8,128)(2,1)S(1)} fusion(bf16[1024,512]{1,0:T(8,128)(2,1)} %all-gather.4.cloned.1.call-done, bf16[1024,512]{1,0:T(8,128)(2,1)S(1)} %bitcast.42), kind=kOutput, calls=%fused_computation | convolution fusion | flops 537133056 | bytes 2621440 | tf_op jit(solution)/shard_map/dot_general | solution.py:196
  65.3 0.0 copy-start.1
  65.3 0.3 copy.14
  65.6 34.8 %all_to_all.16 = bf16[24,88,128]{2,1,0:T(8,128)(2,1)S(1)} all-to-all(bf16[24,88,128]{2,1,0:T(8,128)(2,1)S(1)} %bitcast.38), channel_id=1, replica_groups=mesh['section'=4,'shard'=8,'replica'=24] {'replica'}, dimensions={0} | all-to-all | bytes 1081344 | tf_op jit(solution)/shard_map/all_to_all | solution.py:197
  100.4 0.1 reduce_sum.12
  100.5 0.9 broadcast_in_dim.34
  101.4 9.3 %all-to-all-start.2 = ((bf16[24,88,128]{2,1,0:T(8,128)(2,1)}), bf16[24,88,128]{2,1,0:T(8,128)(2,1)S(1)}, u32[]{:S(2)}, u32[]{:S(2)}) async-start(bf16[24,88,128]{2,1,0:T(8,128)(2,1)} %broadcast_in_dim.34), calls=%async_computation.2 | async-start | bytes 1081344 | tf_op jit(solution)/shard_map/all_to_all | solution.py:199
  110.6 6.5 %collective-permute-start = (bf16[128,4096]{1,0:T(8,128)(2,1)S(1)}, bf16[128,4096]{1,0:T(8,128)(2,1)}, u32[]{:S(2)}, u32[]{:S(2)}) collective-permute-start(bf16[128,4096]{1,0:T(8,128)(2,1)S(1)} %bitcast.44), channel_id=1, source_target_pairs={{0,192},{192,384},{384,576},{1,193},{193,385},{385,577},{2,194},{1... | collective-permute-start | bytes 3145736 | tf_op jit(solution)/shard_map/ppermute | solution.py:19
  117.2 1.9 %collective-permute-start.1 = (bf16[128,4096]{1,0:T(8,128)(2,1)S(1)}, bf16[128,4096]{1,0:T(8,128)(2,1)}, u32[]{:S(2)}, u32[]{:S(2)}) collective-permute-start(bf16[128,4096]{1,0:T(8,128)(2,1)S(1)} %bitcast.46), channel_id=1, source_target_pairs={{192,0},{384,192},{576,384},{193,1},{385,193},{577,385},{194,2},{3... | collective-permute-start | bytes 3145736 | tf_op jit(solution)/shard_map/ppermute | solution.py:19
  119.1 0.6 pad_add_fusion.place_ref
  119.7 0.7 dynamic-slice_multiply_fusion
  120.4 1.0 fusion.1
  121.3 11.9 %collective-permute-done.came_fwd_ref = bf16[128,4096]{1,0:T(8,128)(2,1)} collective-permute-done((bf16[128,4096]{1,0:T(8,128)(2,1)S(1)}, bf16[128,4096]{1,0:T(8,128)(2,1)}, u32[]{:S(2)}, u32[]{:S(2)}) %collective-permute-start) | collective-permute-done | bytes 1048608 | tf_op jit(solution)/shard_map/ppermute | solution.py:19
  133.3 3.9 %collective-permute-done.1.came_bwd_ref = bf16[128,4096]{1,0:T(8,128)(2,1)} collective-permute-done((bf16[128,4096]{1,0:T(8,128)(2,1)S(1)}, bf16[128,4096]{1,0:T(8,128)(2,1)}, u32[]{:S(2)}, u32[]{:S(2)}) %collective-permute-start.1) | collective-permute-done | bytes 1048608 | tf_op jit(solution)/shard_map/ppermute | solution.py:19
  137.2 4.6 %streams.1 = (bf16[128,4096]{1,0:T(8,128)(2,1)}, bf16[128,4096]{1,0:T(8,128)(2,1)}, f32[128,128]{1,0:T(8,128)}) custom-call(bf16[128,4096]{1,0:T(8,128)(2,1)} %bitcast.43, bf16[128,4096]{1,0:T(8,128)(2,1)} %collective-permute-done.came_fwd_ref, bf16[128,4096]{1,0:T(8,128)(2,1)} %bitcast.45, bf16[128,4096]{1,0:T(8,128)(2,1)} %collective-permute-done.1.came_bwd_ref, ...), custom_call_target="tpu_custom_call" | custom-call | tf_op jit(solution)/shard_map/streams/pallas_call | solution.py:92
  141.9 0.1 convert_bitcast_fusion
  142.0 0.3 copy.15
  142.3 0.1 bitcast_multiply_fusion
  142.5 1.3 copy.16
  143.8 8.8 %window.1 = (bf16[128,512]{1,0:T(8,128)(2,1)}, bf16[128,4096]{1,0:T(8,128)(2,1)}) custom-call(bf16[4096,512]{1,0:T(8,128)(2,1)} %bitcast.36, bf16[128,4096]{1,0:T(8,128)(2,1)} %get-tuple-element.11.normed_ref, bf16[128,4096]{1,0:T(8,128)(2,1)} %bitcast.35, bf16[128,4096]{1,0:T(8,128)(2,1)} %get-tuple-element.12.arrived_ref, ...), custom_call_target="tpu_custom_call" | custom-call | tf_op jit(solution)/shard_map/window/pallas_call | solution.py:160
  (11 shorter events, 0.1 us)
Async XLA Ops:
  7.2 56.1 %all-gather.4.cloned.1.call-start = ((), (), s32[]{:S(2)}) async-start(), calls=%async_computation.3 | async-start | bytes 1179648 | tf_op jit(solution)/shard_map/all_gather | solution.py:194
  12.5 131.3 %all-gather.6.cloned.1.call-start = ((), (), s32[]{:S(2)}) async-start(), calls=%async_computation.4 | async-start | bytes 4718592 | tf_op jit(solution)/shard_map/all_gather | solution.py:195
  63.2 47.4 %copy-start = (bf16[1,128,4096]{2,1,0:T(8,128)(2,1)S(1)}, bf16[1,128,4096]{2,1,0:T(8,128)(2,1)}, u32[]{:S(2)}) copy-start(bf16[1,128,4096]{2,1,0:T(8,128)(2,1)} %param.8) | copy-start | bytes 3145732
  63.2 55.8 %copy-start.2 = (s32[1,128]{1,0:T(1,128)S(1)}, s32[1,128]{1,0:T(1,128)}, u32[]{:S(2)}) copy-start(s32[1,128]{1,0:T(1,128)} %param.9) | copy-start | bytes 1540
  65.3 51.9 %copy-start.1 = (bf16[1,128,4096]{2,1,0:T(8,128)(2,1)S(1)}, bf16[1,128,4096]{2,1,0:T(8,128)(2,1)}, u32[]{:S(2)}) copy-start(bf16[1,128,4096]{2,1,0:T(8,128)(2,1)} %param.12) | copy-start | bytes 3145732
  101.4 40.5 %all-to-all-start.2 = ((bf16[24,88,128]{2,1,0:T(8,128)(2,1)}), bf16[24,88,128]{2,1,0:T(8,128)(2,1)S(1)}, u32[]{:S(2)}, u32[]{:S(2)}) async-start(bf16[24,88,128]{2,1,0:T(8,128)(2,1)} %broadcast_in_dim.34), calls=%async_computation.2 | async-start | bytes 1081344 | tf_op jit(solution)/shard_map/all_to_all | solution.py:199
  110.6 22.6 %collective-permute-start = (bf16[128,4096]{1,0:T(8,128)(2,1)S(1)}, bf16[128,4096]{1,0:T(8,128)(2,1)}, u32[]{:S(2)}, u32[]{:S(2)}) collective-permute-start(bf16[128,4096]{1,0:T(8,128)(2,1)S(1)} %bitcast.44), channel_id=1, source_target_pairs={{0,192},{192,384},{384,576},{1,193},{193,385},{385,577},{2,194},{1... | collective-permute-start | bytes 3145736 | tf_op jit(solution)/shard_map/ppermute | solution.py:19
  117.2 20.1 %collective-permute-start.1 = (bf16[128,4096]{1,0:T(8,128)(2,1)S(1)}, bf16[128,4096]{1,0:T(8,128)(2,1)}, u32[]{:S(2)}, u32[]{:S(2)}) collective-permute-start(bf16[128,4096]{1,0:T(8,128)(2,1)S(1)} %bitcast.46), channel_id=1, source_target_pairs={{192,0},{384,192},{576,384},{193,1},{385,193},{577,385},{194,2},{3... | collective-permute-start | bytes 3145736 | tf_op jit(solution)/shard_map/ppermute | solution.py:19
Sparse Core Ops, SparseCore 0:
  12.6 50.5 all-gather.3
  65.6 64.3 all-gather.5
